TPU v7x, 512 devices: a whole 4x8x8 slice. The times are simulated.
512 devices in a mesh: gx: 16 (over z, core), gy: 32 (over x, y).
Axes of the slice: x: 4, y: 8, z: 8, core: 2. Of those that a mesh axis runs over, the one named last changes fastest.
Arguments:
- field: float32 [1024, 12288], P('gx', 'gy'), may hold values from -9 to 9
- decay_x: float32 [1024, 8], P('gx'), may hold values from 0.15 to 0.99999
- decay_y: float32 [1536, 8], P('gy'), may hold values from 0.15 to 0.99999
Outputs:
- smoothed: float32 [1024, 12288], P('gx', 'gy')
All inputs are finite; a program needn't handle non-finite values.
Results may differ from a plain program's by a relative error of at most 0.0003.
Values sent between devices are 32-bit elements; how exact they have to be, the bound alone decides.
No kernel may reach another device: no remote copies, remote signals or barrier semaphores. Data moves between devices by JAX's collectives and lax.ppermute only.
A program may use at most 64 MiB of HBM per device.

v0:
```python
import jax
import jax.numpy as jnp
from jax import lax
from jax.sharding import PartitionSpec as P


def sent_to_all(shard, axis):
    copies = jnp.broadcast_to(shard, (lax.axis_size(axis), *shard.shape))
    return lax.all_to_all(copies, axis, split_axis=0, concat_axis=0, tiled=True)


def collected_together(shard, axis):
    leaves = jax.tree.leaves(shard)
    sequence = sorted(range(len(leaves)), key=lambda k: -leaves[k].size)
    width = (1, *leaves[sequence[0]].shape)[-1]
    lines = [
        jnp.pad(leaves[k].reshape(-1), (0, -leaves[k].size % width)).reshape(-1, width)
        for k in sequence
    ]
    both, at, found = (sent_to_all(jnp.concatenate(lines), axis), 0, {})
    for k, line in zip(sequence, lines):
        piece = both[:, at : at + len(line)].reshape(len(both), -1)
        found[k] = piece[:, : leaves[k].size].reshape(-1, *leaves[k].shape)
        at += len(line)
    numbers = iter(range(len(leaves)))
    return jax.tree.map(lambda _: found[next(numbers)], shard)


def gathered_by_type(shard, axis):
    leaves, found = (jax.tree.leaves(shard), {})
    for leading, a in enumerate(leaves):
        if leading not in found:
            alike = [k for k, b in enumerate(leaves) if b.dtype == a.dtype]
            got = (
                collected_together([leaves[k] for k in alike], axis)
                if len(alike) > 1
                else [sent_to_all(a, axis)]
            )
            for k, b in zip(alike, got):
                found[k] = b
    numbers = iter(range(len(leaves)))
    return jax.tree.map(lambda _: found[next(numbers)], shard)


def joined_by_halves(pieces, combine):
    while len(jax.tree.leaves(pieces)[0]) > 1:
        pieces = jax.vmap(combine)(
            *(jax.tree.map(lambda part: part[side::2], pieces) for side in (0, 1))
        )
    return jax.tree.map(lambda part: part[0], pieces)


def carried_in(shard, axis, combine, identity, reverse):
    devices, mine = (lax.axis_size(axis), lax.axis_index(axis))
    passed = jnp.arange(devices) > mine if reverse else jnp.arange(devices) < mine

    def kept(part, zero, own):
        part = jnp.where(
            passed.reshape(-1, *(1 for _ in own.shape)), part, jnp.asarray(zero, own.dtype)
        )
        return part[::-1] if reverse else part

    pieces = gathered_by_type(shard, axis)
    return joined_by_halves(jax.tree.map(kept, pieces, identity, shard), combine)


def local_operator(decay_factors, backward):
    if backward:
        decay_factors = decay_factors[::-1]
    count = decay_factors.shape[0]
    logs = jnp.log(decay_factors).T
    running = jnp.cumsum(logs, axis=1)
    grid_location = jnp.arange(count)
    lower = (grid_location[:, None] >= grid_location[None, :])[None]
    spread = running[:, :, None] - running[:, None, :]
    matrix = (
        jnp.where(lower, jnp.exp(jnp.where(lower, spread, 0.0)), 0.0)
        * (1.0 - decay_factors).T[:, None, :]
    )
    carried = jnp.exp(running)
    responses = [carried]
    for order in range(3):
        responses.append(
            jnp.einsum("lij,lj->li", matrix, responses[-1], precision=lax.Precision.HIGHEST)
        )
    response = jnp.stack(responses)
    if backward:
        matrix = matrix[:, ::-1, ::-1]
        response = response[:, :, ::-1]
    return (matrix, response)


def section_outputs(values, matrix, axis):
    form = "lij,jwl->iwl" if axis == 0 else "lij,wjl->wil"
    outputs = []
    current = values
    for order in range(4):
        current = jnp.einsum(form, matrix, current, precision=lax.Precision.HIGHEST)
        outputs.append(current)
    return outputs


def end_map(response, edge):
    edges = response[:, :, edge]
    empty = jnp.zeros_like(edges[0])
    rows = [
        jnp.stack(
            [edges[outer - inner] if inner <= outer else empty for inner in range(4)], axis=-1
        )
        for outer in range(4)
    ]
    return jnp.stack(rows, axis=1)


def compose(earlier, later):
    first_map, first_values = earlier
    second_map, second_values = later
    joined = jnp.einsum("lkm,lmn->lkn", second_map, first_map, precision=lax.Precision.HIGHEST)
    moved = (
        jnp.einsum("lkm,mwl->kwl", second_map, first_values, precision=lax.Precision.HIGHEST)
        + second_values
    )
    return (joined, moved)


def correction(response, state, axis):
    form = "mli,mwl->iwl" if axis == 0 else "mli,mwl->wil"
    return jnp.einsum(form, response[::-1], state, precision=lax.Precision.HIGHEST)


def carry_sweep(values, operator, axis, backward):
    matrix, response = operator
    edge = 0 if backward else matrix.shape[1] - 1
    outputs = section_outputs(values, matrix, axis)
    ends = jnp.stack([lax.index_in_dim(section, edge, axis, keepdims=False) for section in outputs])
    mapping = end_map(response, edge)
    start = (jnp.broadcast_to(jnp.eye(4, dtype=jnp.float32), mapping.shape), jnp.zeros_like(ends))
    if axis == 0:
        prefix = carried_in((mapping, ends), "gx", compose, start, backward)
    else:
        prefix = carried_in((mapping, ends), "gy", compose, start, backward)
    return outputs[3] + correction(response, prefix[1], axis)


def body(field, decay_x, decay_y):
    rows_x = decay_x.shape[0]
    levels = decay_x.shape[1]
    rows_y = decay_y.shape[0]
    grid = field.reshape(rows_x, rows_y, levels)
    forward_x = local_operator(decay_x, False)
    backward_x = local_operator(decay_x, True)
    forward_y = local_operator(decay_y, False)
    backward_y = local_operator(decay_y, True)
    grid = carry_sweep(grid, forward_x, 0, False)
    grid = carry_sweep(grid, backward_x, 0, True)
    grid = carry_sweep(grid, forward_y, 1, False)
    grid = carry_sweep(grid, backward_y, 1, True)
    return grid.reshape(rows_x, rows_y * levels)


def solution(mesh):
    placed = (P("gx", "gy"), P("gx", None), P("gy", None))
    return jax.shard_map(body, mesh=mesh, in_specs=placed, out_specs=P("gx", "gy"), check_vma=False)
```

profile of v0, /device:TPU:8, one launch (start us, length us, event | category | flops | bytes accessed | tf_op | source)
XLA Modules:
  0.0 121.2 jit_solution(9710195405224753319)
XLA Ops:
  0.0 0.7 copy-done
  0.9 1.0 copy.139
  1.9 0.7 convolution_bitcast_fusion.11
  2.6 0.6 convolution_bitcast_fusion.10
  3.3 0.6 convolution_bitcast_fusion.9
  3.9 0.6 convolution_bitcast_fusion.8
  4.9 0.6 fusion.31
  5.5 0.6 fusion.30
  6.2 0.6 fusion.29
  8.6 0.7 broadcast_in_dim.179
  9.3 10.4 %all-to-all-start = ((f32[16,208,8]{1,2,0:T(8,128)}), f32[16,208,8]{1,2,0:T(8,128)S(1)}, u32[]{:S(2)}, u32[]{:S(2)}) async-start(f32[16,208,8]{1,2,0:T(8,128)} %broadcast_in_dim.179), calls=%async_computation | async-start | bytes 262144 | tf_op jit(solution)/shard_map/all_to_all | solution.py:9
  19.8 0.7 copy-done.1
  21.3 0.5 fusion.47
  21.8 0.5 fusion.46
  22.4 0.5 fusion.45
  23.3 0.5 fusion.115
  23.8 0.5 fusion.114
  24.4 0.5 fusion.113
  26.2 0.6 fusion.51
  26.9 0.6 fusion.50
  27.5 0.6 fusion.49
  29.5 0.4 copy.145
  30.3 0.6 fusion.69
  30.9 0.6 fusion.4
  31.5 0.4 fusion.181
  31.8 0.3 fusion.11
  32.8 0.5 fusion.3
  33.3 0.5 convolution_bitcast_fusion.7
  33.8 0.5 convolution_bitcast_fusion.6
  34.4 0.5 convolution_bitcast_fusion.5
  34.9 0.5 convolution_bitcast_fusion.4
  36.0 0.7 broadcast_in_dim.184
  36.6 7.2 %all-to-all-start.1 = ((f32[16,208,8]{1,2,0:T(8,128)}), f32[16,208,8]{1,2,0:T(8,128)S(1)}, u32[]{:S(2)}, u32[]{:S(2)}) async-start(f32[16,208,8]{1,2,0:T(8,128)} %broadcast_in_dim.184), calls=%async_computation.1 | async-start | bytes 262144 | tf_op jit(solution)/shard_map/all_to_all | solution.py:9
  44.2 8.3 %all-to-all-done.1 = f32[16,208,8]{1,2,0:T(8,128)S(1)} async-done(((f32[16,208,8]{1,2,0:T(8,128)}), f32[16,208,8]{1,2,0:T(8,128)S(1)}, u32[]{:S(2)}, u32[]{:S(2)}) %all-to-all-start.1) | async-done | bytes 106528 | tf_op jit(solution)/shard_map/all_to_all | solution.py:9
  53.1 0.4 copy.153
  53.6 0.5 fusion.58
  54.1 0.4 fusion.178
  54.5 0.6 fusion.7
  56.1 0.5 fusion.2
  56.6 0.4 convolution_bitcast_fusion.3
  57.0 0.4 fusion.48
  57.3 0.4 fusion.41
  57.7 0.4 fusion.39
  58.5 0.8 broadcast_in_dim.189
  59.3 10.2 %all-to-all-start.2 = ((f32[32,272,8]{1,2,0:T(8,128)}), f32[32,272,8]{1,2,0:T(8,128)S(1)}, u32[]{:S(2)}, u32[]{:S(2)}) async-start(f32[32,272,8]{1,2,0:T(8,128)} %broadcast_in_dim.189), calls=%async_computation.2 | async-start | bytes 786432 | tf_op jit(solution)/shard_map/all_to_all | solution.py:9
  70.0 14.9 %all-to-all-done.2 = f32[32,272,8]{1,2,0:T(8,128)S(1)} async-done(((f32[32,272,8]{1,2,0:T(8,128)}), f32[32,272,8]{1,2,0:T(8,128)S(1)}, u32[]{:S(2)}, u32[]{:S(2)}) %all-to-all-start.2) | async-done | bytes 278560 | tf_op jit(solution)/shard_map/all_to_all | solution.py:9
  85.3 0.6 copy.166
  86.3 1.0 fusion.26
  87.2 1.0 fusion.1
  88.2 0.6 fusion.55
  88.8 0.6 fusion.5
  89.4 0.4 fusion.175
  90.7 0.5 fusion.210
  93.0 0.8 broadcast_in_dim.194
  93.8 5.2 %all-to-all-start.3 = ((f32[32,272,8]{1,2,0:T(8,128)}), f32[32,272,8]{1,2,0:T(8,128)S(1)}, u32[]{:S(2)}, u32[]{:S(2)}) async-start(f32[32,272,8]{1,2,0:T(8,128)} %broadcast_in_dim.194), calls=%async_computation.3 | async-start | bytes 786432 | tf_op jit(solution)/shard_map/all_to_all | solution.py:9
  99.1 14.7 %all-to-all-done.3 = f32[32,272,8]{1,2,0:T(8,128)S(1)} async-done(((f32[32,272,8]{1,2,0:T(8,128)}), f32[32,272,8]{1,2,0:T(8,128)S(1)}, u32[]{:S(2)}, u32[]{:S(2)}) %all-to-all-start.3) | async-done | bytes 278560 | tf_op jit(solution)/shard_map/all_to_all | solution.py:9
  114.5 0.6 copy.181
  115.4 0.9 fusion.24
  116.3 0.6 fusion.52
  116.9 1.0 fusion
  117.9 0.6 fusion.6
  118.5 0.4 fusion.172
  119.8 0.5 fusion.208
  120.5 0.8 copy.186
  (160 shorter events, 15.9 us)
Async XLA Ops:
  0.0 0.7 copy-start
  9.3 20.0 %all-to-all-start = ((f32[16,208,8]{1,2,0:T(8,128)}), f32[16,208,8]{1,2,0:T(8,128)S(1)}, u32[]{:S(2)}, u32[]{:S(2)}) async-start(f32[16,208,8]{1,2,0:T(8,128)} %broadcast_in_dim.179), calls=%async_computation | async-start | bytes 262144 | tf_op jit(solution)/shard_map/all_to_all | solution.py:9
  19.8 0.7 copy-start.1
  36.6 15.9 %all-to-all-start.1 = ((f32[16,208,8]{1,2,0:T(8,128)}), f32[16,208,8]{1,2,0:T(8,128)S(1)}, u32[]{:S(2)}, u32[]{:S(2)}) async-start(f32[16,208,8]{1,2,0:T(8,128)} %broadcast_in_dim.184), calls=%async_computation.1 | async-start | bytes 262144 | tf_op jit(solution)/shard_map/all_to_all | solution.py:9
  59.3 25.7 %all-to-all-start.2 = ((f32[32,272,8]{1,2,0:T(8,128)}), f32[32,272,8]{1,2,0:T(8,128)S(1)}, u32[]{:S(2)}, u32[]{:S(2)}) async-start(f32[32,272,8]{1,2,0:T(8,128)} %broadcast_in_dim.189), calls=%async_computation.2 | async-start | bytes 786432 | tf_op jit(solution)/shard_map/all_to_all | solution.py:9
  93.8 20.1 %all-to-all-start.3 = ((f32[32,272,8]{1,2,0:T(8,128)}), f32[32,272,8]{1,2,0:T(8,128)S(1)}, u32[]{:S(2)}, u32[]{:S(2)}) async-start(f32[32,272,8]{1,2,0:T(8,128)} %broadcast_in_dim.194), calls=%async_computation.3 | async-start | bytes 786432 | tf_op jit(solution)/shard_map/all_to_all | solution.py:9
where the time goes:
time: 122 us; the launch traced here: 121 us
  waiting for transfers between devices  38 us (31%)
  starting transfers between devices  33 us (27%)
  matrix products  30.1 us (25%)
  local copies, waits for them, and re-layouts  15.7 us (13%)
  other arithmetic  3.45 us (3%)
    all_to_all x4, waiting for transfers between devices, sent_to_all(): return lax.all_to_all(copies, axis, split_axis=0, concat_axis=0, tiled=True)  38 us
    all_to_all x4, starting transfers between devices, sent_to_all(): return lax.all_to_all(copies, axis, split_axis=0, concat_axis=0, tiled=True)  33 us
    dot_general x18, matrix products, compose(): jnp.einsum('lkm,mwl->kwl', second_map, first_values, precision=lax.Precis...  7.39 us
    dot_general x16, matrix products, section_outputs(): current = jnp.einsum(form, matrix, current, precision=lax.Precision.HIGHEST)  7.39 us
    dot_general x12, matrix products, local_operator(): jnp.einsum('lij,lj->li', matrix, responses[-1], precision=lax.Precision.H...  7.02 us
    dot_general x10, matrix products, compose(): jnp.einsum('lkm,lmn->lkn', second_map, first_map, precision=lax.Precision...  5.54 us
    slice x16, local copies, waits for them, and re-layouts, end_map(): edges[outer - inner]  2.95 us
    broadcast_in_dim x4, local copies, waits for them, and re-layouts, sent_to_all(): copies = jnp.broadcast_to(shard, (lax.axis_size(axis), *shard.shape))  2.87 us
  transfers between devices with their start and end apart: 4, of which 3 were waited for; matrix products, arithmetic and copies ran while one was open for 8% of the time, Pallas kernels for 0%

commit v1 on v0

v1 whole, which is shorter than its diff:
```python
import jax
import jax.numpy as jnp
from jax import lax
from jax.experimental import pallas as pl
from jax.experimental.pallas import tpu as pltpu
from jax.sharding import PartitionSpec as P

F32 = jnp.float32
LANES = 128
VMEM = pltpu.MemorySpace.VMEM


def iota(shape, dim):
    return lax.broadcasted_iota(jnp.int32, shape, dim)


def take_lanes(values, lanes):
    return jnp.take_along_axis(values, jnp.broadcast_to(lanes, values.shape), axis=1)


def cascade(states, value, decay, gain):
    moved = []
    for state in states:
        value = decay * state + gain * value
        moved.append(value)
    return moved


def toeplitz(column, states):
    return [
        sum((column[row - k] * states[k] for k in range(1, row + 1)), column[row] * states[0])
        for row in range(4)
    ]


def sweep(steps, states, load, decay, gain, store, reverse):
    for step in reversed(range(steps)) if reverse else range(steps):
        states = cascade(states, load(step), decay(step), gain(step))
        if store is not None:
            store(step, states[3])
    return states


def x_ends(field_ref, decay_ref, sent_ref, grid_ref, a_ref, wide_ref, out_ref):
    steps, levels = decay_ref.shape
    a_ref[:, :levels] = decay_ref[...]
    periodic = take_lanes(a_ref[...], iota((steps, LANES), 1) % levels)
    a_ref[...] = periodic
    tiles = field_ref.shape[1] // LANES
    for tile in range(tiles):
        grid_ref[:, tile, :] = field_ref[:, tile * LANES : (tile + 1) * LANES]
    grid_ref[:, tiles, :] = jnp.zeros((steps, LANES), F32)
    row, group = (iota((4, LANES), 0), iota((4, LANES), 1) // levels)
    unit = [((row == tiles) & (group == k)).astype(F32) for k in range(8)]
    load_a = lambda i: a_ref[pl.ds(i, 1), :]
    gain = lambda i: 1.0 - a_ref[pl.ds(i, 1), :]

    def keep(i, value):
        out_ref[i] = value

    ahead = sweep(steps, unit[:4], lambda i: grid_ref[i], load_a, gain, keep, False)
    back = sweep(steps, unit[4:], lambda i: out_ref[i], load_a, gain, None, True)
    ends = ahead + back
    for k in range(8):
        wide_ref[4 * k : 4 * k + 4, :] = ends[k]
    both = wide_ref[...]
    for device in range(sent_ref.shape[0]):
        sent_ref[device] = both


def y_decays(decay_ref, a_ref):
    steps, levels = decay_ref.shape
    padded = decay_ref[...]
    spread = jnp.broadcast_to(padded[:, None, :], (steps, levels, levels))
    own = iota(spread.shape, 1) == iota(spread.shape, 2)
    column = jnp.sum(jnp.where(own, spread, 0.0), axis=2, keepdims=True)
    a_ref[...] = jnp.broadcast_to(column, (steps, levels, LANES)).reshape(steps * levels, LANES)


def x_apply_y_ends(
    got_ref, grid_ref, ax_ref, ay_ref, sent_ref, wide_ref, maps_ref, s_ref, t_ref, z_ref, out_ref
):
    devices, steps = (16, grid_ref.shape[0])
    rows = got_ref.shape[0] // devices
    levels = 8
    mine = lax.axis_index("gx")
    found = got_ref[pl.ds(3, devices * 8, stride=4), :]
    lane = iota(found.shape, 1) % levels
    for k in range(5):
        maps_ref[k] = take_lanes(found, lane + 8 * k)

    def end(m, k):
        return got_ref[rows * m + 4 * k : rows * m + 4 * k + 4, :]

    def entry(k, m, value):
        return maps_ref[k, pl.ds(8 * m + value, 1), :]

    zero = jnp.zeros((4, LANES), F32)
    states = [zero] * 4
    for m in range(devices):
        for k in range(4):
            s_ref[m, k] = states[k]
        if m < devices - 1:
            moved = toeplitz([entry(0, m, k) for k in range(4)], states)
            states = [moved[k] + end(m, k) for k in range(4)]
    states = [zero] * 4
    for m in reversed(range(devices)):
        for k in range(4):
            t_ref[m, k] = states[k]
        if m > 0:
            moved = toeplitz([entry(4, m, 4 + k) for k in range(4)], states)
            turned = [
                sum(entry(k, m, 4 + r) * s_ref[m, k] for k in range(4)) + end(m, 4 + r)
                for r in range(4)
            ]
            states = [moved[k] + turned[k] for k in range(4)]
    load_a = lambda i: ax_ref[pl.ds(i, 1), :]
    gain = lambda i: 1.0 - ax_ref[pl.ds(i, 1), :]

    def keep(i, value):
        z_ref[i] = value

    start = [s_ref[mine, k] for k in range(4)]
    sweep(steps, start, lambda i: grid_ref[i], load_a, gain, keep, False)
    start = [t_ref[mine, k] for k in range(4)]
    sweep(steps, start, lambda i: z_ref[i], load_a, gain, keep, True)
    wide_ref[...] = jnp.zeros(wide_ref.shape, F32)
    for tile in range(3):
        wide_ref[tile * LANES : (tile + 1) * LANES, :steps] = z_ref[:, tile, :].T

    lane = iota((8, LANES), 1)
    unit = [(lane == steps + k).astype(F32) for k in range(8)]
    count = ay_ref.shape[0] // 8
    load = lambda ref: lambda i: ref[8 * i : 8 * i + 8, :]
    load_a = load(ay_ref)
    gain = lambda i: 1.0 - load_a(i)

    def keep_y(i, value):
        out_ref[8 * i : 8 * i + 8, :] = value

    ahead = sweep(count, unit[:4], load(wide_ref), load_a, gain, keep_y, False)
    back = sweep(count, unit[4:], load(out_ref), load_a, gain, None, True)
    low = lane < steps
    tiles = [jnp.where(low, ahead[k], pltpu.roll(back[k], steps, 1)) for k in range(4)]
    packed = jnp.zeros((8, LANES), F32)
    for k in range(4):
        for shift, ends in ((0, back), (8, ahead)):
            at = 16 * k + shift
            moved = pltpu.roll(ends[k], (at - steps) % LANES, 1)
            packed = jnp.where((lane >= at) & (lane < at + 8), moved, packed)
    tiles.append(packed)
    for device in range(sent_ref.shape[0]):
        for k in range(5):
            sent_ref[device, k] = tiles[k]


def y_apply(got_ref, wide_ref, ay_ref, field_ref, s_ref, t_ref, z_ref):
    devices = got_ref.shape[0]
    mine = lax.axis_index("gy")
    half = LANES // 2

    def entry(packed, at):
        return jnp.broadcast_to(packed[:, at : at + 1], (8, LANES))

    zero = jnp.zeros((8, LANES), F32)
    states = [zero] * 4
    for m in range(devices):
        for k in range(4):
            s_ref[m, k] = states[k]
        if m < devices - 1:
            packed = got_ref[m, 4]
            moved = toeplitz([entry(packed, 16 * k + 8) for k in range(4)], states)
            states = [moved[k] + got_ref[m, k] for k in range(4)]
    states = [zero] * 4
    for m in reversed(range(devices)):
        for k in range(4):
            t_ref[m, k] = states[k]
        if m > 0:
            packed = got_ref[m, 4]
            moved = toeplitz([entry(packed, 16 * k + 4) for k in range(4)], states)
            turned = [
                sum(entry(packed, 16 * r + k) * s_ref[m, k] for k in range(4))
                + pltpu.roll(got_ref[m, r], half, 1)
                for r in range(4)
            ]
            states = [moved[k] + turned[k] for k in range(4)]
    count = ay_ref.shape[0] // 8
    load = lambda ref: lambda i: ref[8 * i : 8 * i + 8, :]
    load_a = load(ay_ref)
    gain = lambda i: 1.0 - load_a(i)

    def keep(i, value):
        z_ref[8 * i : 8 * i + 8, :] = value

    start = [s_ref[mine, k] for k in range(4)]
    sweep(count, start, load(wide_ref), load_a, gain, keep, False)
    start = [t_ref[mine, k] for k in range(4)]
    sweep(count, start, load(z_ref), load_a, gain, keep, True)
    for tile in range(3):
        turned = z_ref[tile * LANES : (tile + 1) * LANES, :].T
        field_ref[:, tile * LANES : (tile + 1) * LANES] = turned[:half]


def call(kernel, outs, scratch, *args):
    whole = pl.BlockSpec(memory_space=VMEM)
    return pl.pallas_call(
        kernel,
        out_shape=[jax.ShapeDtypeStruct(shape, F32) for shape in outs],
        in_specs=[whole] * len(args),
        out_specs=[whole] * len(outs),
        scratch_shapes=[pltpu.VMEM(shape, F32) for shape in scratch],
    )(*args)


def body(field, decay_x, decay_y):
    along_x, along_y = (lax.axis_size("gx"), lax.axis_size("gy"))
    rows, columns = field.shape
    count = decay_y.shape[0]
    sent, grid, ax = call(
        x_ends,
        [(along_x, 32, LANES), (rows, 4, LANES), (rows, LANES)],
        [(32, LANES), (rows, 4, LANES)],
        field,
        decay_x,
    )
    got = lax.all_to_all(sent, "gx", 0, 0, tiled=True)
    (ay,) = call(y_decays, [(columns, LANES)], [], decay_y)
    sent, wide = call(
        x_apply_y_ends,
        [(along_y, 5, 8, LANES), (columns, LANES)],
        [
            (5, along_x * 8, LANES),
            (along_x, 4, 4, LANES),
            (along_x, 4, 4, LANES),
            (rows, 4, LANES),
            (columns, LANES),
        ],
        got.reshape(along_x * 32, LANES),
        grid,
        ax,
        ay,
    )
    got = lax.all_to_all(sent, "gy", 0, 0, tiled=True)
    (out,) = call(
        y_apply,
        [(rows, columns)],
        [(along_y, 4, 8, LANES), (along_y, 4, 8, LANES), (columns, LANES)],
        got,
        wide,
        ay,
    )
    return out


def solution(mesh):
    placed = (P("gx", "gy"), P("gx", None), P("gy", None))
    return jax.shard_map(body, mesh=mesh, in_specs=placed, out_specs=P("gx", "gy"), check_vma=False)
```

time: 122 us -> 64.4 us (0.53)
  blocking collectives: 0 us -> 31.5 us
  matrix products: 30.1 us -> 0 us
  waiting for transfers between devices: 38 us -> 8.9 us
  starting transfers between devices: 33 us -> 10.6 us
  local copies, waits for them, and re-layouts: 15.7 us -> 2.78 us
  Pallas kernels: 0 us -> 10.2 us
  other arithmetic: 3.45 us -> 0 us
    all_to_all x0 -> x1, blocking collectives: none -> 31.5 us  [body(): got = lax.all_to_all(sent, 'gy', 0, 0, tiled=True)]
    dot_general x60 -> x0, matrix products: 29.4 us -> none  [the longest x18 7.39 us: compose(): jnp.einsum('lkm,mwl->kwl', second_map, first_values, precision=lax.Precis...]
    all_to_all x4 -> x1, waiting for transfers between devices: 38 us -> 8.9 us  [body(): got = lax.all_to_all(sent, 'gx', 0, 0, tiled=True)]
    all_to_all x4 -> x1, starting transfers between devices: 33 us -> 10.6 us  [body(): got = lax.all_to_all(sent, 'gx', 0, 0, tiled=True)]
    pallas_call x0 -> x4, Pallas kernels: none -> 10.2 us  [call(): pl.pallas_call(kernel, out_shape=[jax.ShapeDtypeStruct(shape, F32) for sh...]
    slice x38 -> x0, local copies, waits for them, and re-layouts: 3.79 us -> none  [the longest x16 2.95 us: end_map(): edges[outer - inner]]
    another operation x25 -> x0, local copies, waits for them, and re-layouts: 3.52 us -> none  [the longest x8 2.77 us: collected_together(): found[k] = piece[:, :leaves[k].size].reshape(-1, *leaves[k].shape)]
    broadcast_in_dim x4 -> x0, local copies, waits for them, and re-layouts: 2.87 us -> none  [sent_to_all(): copies = jnp.broadcast_to(shard, (lax.axis_size(axis), *shard.shape))]
  transfers between devices with their start and end apart: 4 -> 1, of which waited for: 3 -> 1; matrix products, arithmetic and copies ran while one was open for 8% -> 1% of each run, Pallas kernels for 0% -> 2%
where the time goes in v1:
time: 64.4 us; the launch traced here: 63.9 us
  blocking collectives  31.5 us (49%)
  starting transfers between devices  10.6 us (16%)
  Pallas kernels  10.2 us (16%)
  waiting for transfers between devices  8.9 us (14%)
  local copies, waits for them, and re-layouts  2.78 us (4%)
    all_to_all x1, blocking collectives, body(): got = lax.all_to_all(sent, 'gy', 0, 0, tiled=True)  31.5 us
    all_to_all x1, starting transfers between devices, body(): got = lax.all_to_all(sent, 'gx', 0, 0, tiled=True)  10.6 us
    pallas_call x4, Pallas kernels, call(): pl.pallas_call(kernel, out_shape=[jax.ShapeDtypeStruct(shape, F32) for sh...  10.2 us
    all_to_all x1, waiting for transfers between devices, body(): got = lax.all_to_all(sent, 'gx', 0, 0, tiled=True)  8.9 us
    unnamed x6, local copies, waits for them, and re-layouts  2.78 us
  transfers between devices with their start and end apart: 1, of which 1 were waited for; matrix products, arithmetic and copies ran while one was open for 1% of the time, Pallas kernels for 2%

profile of v1, /device:TPU:8, one launch (start us, length us, event | category | flops | bytes accessed | tf_op | source)
XLA Modules:
  0.0 63.9 jit_solution(10935712436678010578)
XLA Ops:
  0.0 1.4 %copy.4.decay_ref = f32[64,8]{1,0:T(8,128)} copy(f32[64,8]{0,1:T(8,128)} %param.4) | data formatting | bytes 4096 | tf_op args[1]
  1.4 2.0 %shard_map.37 = (f32[16,32,128]{2,1,0:T(8,128)}, f32[64,4,128]{2,1,0:T(4,128)}, f32[64,128]{1,0:T(8,128)}) custom-call(f32[64,384]{1,0:T(8,128)} %field_ref.1, f32[64,8]{1,0:T(8,128)} %copy.4.decay_ref), custom_call_target="tpu_custom_call" | custom-call | tf_op jit(solution)/shard_map/pallas_call | solution.py:206
  3.4 0.0 copy-start.1
  3.4 10.6 %all-to-all-start = ((f32[16,32,128]{2,1,0:T(8,128)}), f32[16,32,128]{2,1,0:T(8,128)S(1)}, u32[]{:S(2)}, u32[]{:S(2)}) async-start(f32[16,32,128]{2,1,0:T(8,128)} %get-tuple-element.10), calls=%async_computation | async-start | bytes 524288 | tf_op jit(solution)/shard_map/all_to_all | solution.py:226
  14.0 0.0 copy-done.1
  14.0 0.7 %copy.5.decay_ref = f32[48,8]{1,0:T(8,128)} copy(f32[48,8]{0,1:T(8,128)S(1)} %copy-done.1) | data formatting | bytes 3072 | tf_op args[2]
  14.7 1.6 %shard_map.38.ay_ref = f32[384,128]{1,0:T(8,128)} custom-call(f32[48,8]{1,0:T(8,128)} %copy.5.decay_ref), custom_call_target="tpu_custom_call" | custom-call | tf_op jit(solution)/shard_map/pallas_call | solution.py:206
  16.2 8.9 %all-to-all-done = f32[16,32,128]{2,1,0:T(8,128)S(1)} async-done(((f32[16,32,128]{2,1,0:T(8,128)}), f32[16,32,128]{2,1,0:T(8,128)S(1)}, u32[]{:S(2)}, u32[]{:S(2)}) %all-to-all-start) | async-done | bytes 262176 | tf_op jit(solution)/shard_map/all_to_all | solution.py:226
  25.1 0.0 copy-start
  25.1 0.7 %copy-done = f32[16,32,128]{2,1,0:T(8,128)} copy-done((f32[16,32,128]{2,1,0:T(8,128)}, f32[16,32,128]{2,1,0:T(8,128)S(1)}, u32[]{:S(2)}) %copy-start) | copy-done | bytes 262168
  25.8 3.0 %shard_map.39 = (f32[32,5,8,128]{3,2,1,0:T(8,128)}, f32[384,128]{1,0:T(8,128)}) custom-call(f32[512,128]{1,0:T(8,128)} %bitcast.1, f32[64,4,128]{2,1,0:T(4,128)} %get-tuple-element.11.grid_ref, f32[64,128]{1,0:T(8,128)} %get-tuple-element.12.ax_ref, f32[384,128]{1,0:T(8,128)} %shard_map.38.ay_ref), custom_call_target="tpu_custom_call" | custom-call | tf_op jit(solution)/shard_map/pallas_call | solution.py:206
  28.8 31.5 %all_to_all.10.got_ref = f32[32,5,8,128]{3,2,1,0:T(8,128)} all-to-all(f32[32,5,8,128]{3,2,1,0:T(8,128)} %get-tuple-element.13), channel_id=1, replica_groups=mesh['gx'=16,'gy'=32] {'gy'}, dimensions={0} | all-to-all | bytes 1310720 | tf_op jit(solution)/shard_map/all_to_all | solution.py:243
  60.3 3.6 %shard_map.40 = f32[64,384]{1,0:T(8,128)} custom-call(f32[32,5,8,128]{3,2,1,0:T(8,128)} %all_to_all.10.got_ref, f32[384,128]{1,0:T(8,128)} %get-tuple-element.14.wide_ref, f32[384,128]{1,0:T(8,128)} %shard_map.38.ay_ref), custom_call_target="tpu_custom_call" | custom-call | tf_op jit(solution)/shard_map/pallas_call | solution.py:206
Async XLA Ops:
  3.4 10.6 %copy-start.1 = (f32[48,8]{0,1:T(8,128)S(1)}, f32[48,8]{0,1:T(8,128)}, u32[]{:S(2)}) copy-start(f32[48,8]{0,1:T(8,128)} %param.5) | copy-start | bytes 4612
  3.4 21.7 %all-to-all-start = ((f32[16,32,128]{2,1,0:T(8,128)}), f32[16,32,128]{2,1,0:T(8,128)S(1)}, u32[]{:S(2)}, u32[]{:S(2)}) async-start(f32[16,32,128]{2,1,0:T(8,128)} %get-tuple-element.10), calls=%async_computation | async-start | bytes 524288 | tf_op jit(solution)/shard_map/all_to_all | solution.py:226
  25.1 0.7 %copy-start = (f32[16,32,128]{2,1,0:T(8,128)}, f32[16,32,128]{2,1,0:T(8,128)S(1)}, u32[]{:S(2)}) copy-start(f32[16,32,128]{2,1,0:T(8,128)S(1)} %all-to-all-done) | copy-start | bytes 786436

commit v2 on v1

--- a/solution.py
+++ b/solution.py
@@ -1,3 +1,5 @@
+import functools
+
 import jax
 import jax.numpy as jnp
 from jax import lax
@@ -42,10 +44,8 @@
 
 
 def x_ends(field_ref, decay_ref, sent_ref, grid_ref, a_ref, wide_ref, out_ref):
-    steps, levels = decay_ref.shape
-    a_ref[:, :levels] = decay_ref[...]
-    periodic = take_lanes(a_ref[...], iota((steps, LANES), 1) % levels)
-    a_ref[...] = periodic
+    levels, steps = decay_ref.shape
+    a_ref[...] = jnp.concatenate([decay_ref[...]] * (LANES // levels), axis=0).T
     tiles = field_ref.shape[1] // LANES
     for tile in range(tiles):
         grid_ref[:, tile, :] = field_ref[:, tile * LANES : (tile + 1) * LANES]
@@ -69,23 +69,58 @@
 
 
 def y_decays(decay_ref, a_ref):
-    steps, levels = decay_ref.shape
-    padded = decay_ref[...]
-    spread = jnp.broadcast_to(padded[:, None, :], (steps, levels, levels))
-    own = iota(spread.shape, 1) == iota(spread.shape, 2)
-    column = jnp.sum(jnp.where(own, spread, 0.0), axis=2, keepdims=True)
-    a_ref[...] = jnp.broadcast_to(column, (steps, levels, LANES)).reshape(steps * levels, LANES)
+    decays = decay_ref[...]
+    for step in range(decays.shape[1]):
+        a_ref[8 * step : 8 * step + 8, :] = lane_of(decays, step)
+
+
+def lane_of(values, at):
+    return jnp.broadcast_to(values[:, at : at + 1], (8, LANES))
+
+
+def pack(ahead, back, lane):
+    half = LANES // 2
+    tiles = [jnp.where(lane < half, ahead[k], pltpu.roll(back[k], half, 1)) for k in range(4)]
+    packed = jnp.zeros((8, LANES), F32)
+    for k in range(4):
+        for shift, ends in ((0, back), (8, ahead)):
+            at = 16 * k + shift
+            moved = pltpu.roll(ends[k], (at - half) % LANES, 1)
+            packed = jnp.where((lane >= at) & (lane < at + 8), moved, packed)
+    return [*tiles, packed]
+
+
+def chained(got_ref, ahead, back, s_ref, t_ref):
+    blocks, half = (got_ref.shape[0], LANES // 2)
+    low = iota((8, LANES), 1) < half
+    for m in range(blocks):
+        packed = got_ref[m, 4]
+        for k in range(4):
+            s_ref[m, k] = ahead[k]
+        moved = toeplitz([lane_of(packed, 16 * k + 8) for k in range(4)], ahead)
+        ahead = [moved[k] + jnp.where(low, got_ref[m, k], 0.0) for k in range(4)]
+    for m in reversed(range(blocks)):
+        packed = got_ref[m, 4]
+        for k in range(4):
+            t_ref[m, k] = back[k]
+        moved = toeplitz([lane_of(packed, 16 * k + 4) for k in range(4)], back)
+        turned = [
+            sum(lane_of(packed, 16 * r + k) * s_ref[m, k] for k in range(4))
+            + jnp.where(low, pltpu.roll(got_ref[m, r], half, 1), 0.0)
+            for r in range(4)
+        ]
+        back = [moved[k] + turned[k] for k in range(4)]
+    return ahead, back
 
 
 def x_apply_y_ends(
     got_ref, grid_ref, ax_ref, ay_ref, sent_ref, wide_ref, maps_ref, s_ref, t_ref, z_ref, out_ref
 ):
-    devices, steps = (16, grid_ref.shape[0])
-    rows = got_ref.shape[0] // devices
-    levels = 8
+    steps = grid_ref.shape[0]
+    devices, rows = (s_ref.shape[0], 32)
     mine = lax.axis_index("gx")
     found = got_ref[pl.ds(3, devices * 8, stride=4), :]
-    lane = iota(found.shape, 1) % levels
+    lane = iota(found.shape, 1) % 8
     for k in range(5):
         maps_ref[k] = take_lanes(found, lane + 8 * k)
 
@@ -140,50 +175,43 @@
 
     ahead = sweep(count, unit[:4], load(wide_ref), load_a, gain, keep_y, False)
     back = sweep(count, unit[4:], load(out_ref), load_a, gain, None, True)
-    low = lane < steps
-    tiles = [jnp.where(low, ahead[k], pltpu.roll(back[k], steps, 1)) for k in range(4)]
-    packed = jnp.zeros((8, LANES), F32)
-    for k in range(4):
-        for shift, ends in ((0, back), (8, ahead)):
-            at = 16 * k + shift
-            moved = pltpu.roll(ends[k], (at - steps) % LANES, 1)
-            packed = jnp.where((lane >= at) & (lane < at + 8), moved, packed)
-    tiles.append(packed)
+    tiles = pack(ahead, back, lane)
     for device in range(sent_ref.shape[0]):
         for k in range(5):
             sent_ref[device, k] = tiles[k]
 
 
-def y_apply(got_ref, wide_ref, ay_ref, field_ref, s_ref, t_ref, z_ref):
-    devices = got_ref.shape[0]
-    mine = lax.axis_index("gy")
+def y_join(got_ref, sent_ref, mine_ref, s_ref, t_ref):
+    blocks = got_ref.shape[0]
+    lane = iota((8, LANES), 1)
+    unit = [(lane == LANES // 2 + k).astype(F32) for k in range(8)]
+    ahead, back = chained(got_ref, unit[:4], unit[4:], s_ref, t_ref)
+    tiles = pack(ahead, back, lane)
+    for device in range(sent_ref.shape[0]):
+        for k in range(5):
+            sent_ref[device, k] = tiles[k]
+    mine = lax.axis_index("gy") % blocks
+    for k in range(4):
+        mine_ref[k] = s_ref[mine, k]
+        mine_ref[4 + k] = t_ref[mine, k]
+
+
+def y_apply(got_ref, mine_ref, wide_ref, ay_ref, field_ref, s_ref, t_ref, z_ref, *, blocks):
     half = LANES // 2
-
-    def entry(packed, at):
-        return jnp.broadcast_to(packed[:, at : at + 1], (8, LANES))
-
-    zero = jnp.zeros((8, LANES), F32)
-    states = [zero] * 4
-    for m in range(devices):
-        for k in range(4):
-            s_ref[m, k] = states[k]
-        if m < devices - 1:
-            packed = got_ref[m, 4]
-            moved = toeplitz([entry(packed, 16 * k + 8) for k in range(4)], states)
-            states = [moved[k] + got_ref[m, k] for k in range(4)]
-    states = [zero] * 4
-    for m in reversed(range(devices)):
-        for k in range(4):
-            t_ref[m, k] = states[k]
-        if m > 0:
-            packed = got_ref[m, 4]
-            moved = toeplitz([entry(packed, 16 * k + 4) for k in range(4)], states)
-            turned = [
-                sum(entry(packed, 16 * r + k) * s_ref[m, k] for k in range(4))
-                + pltpu.roll(got_ref[m, r], half, 1)
-                for r in range(4)
-            ]
-            states = [moved[k] + turned[k] for k in range(4)]
+    zero = [jnp.zeros((8, LANES), F32)] * 4
+    chained(got_ref, zero, zero, s_ref, t_ref)
+    mine = lax.axis_index("gy") // blocks
+    ahead = [s_ref[mine, k] for k in range(4)]
+    back = [t_ref[mine, k] for k in range(4)]
+
+    def entered(k, starts):
+        found = mine_ref[k]
+        return found + sum(lane_of(found, half + at) * state for at, state in starts)
+
+    first = [(k, ahead[k]) for k in range(4)]
+    both = first + [(4 + k, back[k]) for k in range(4)]
+    ahead = [entered(k, first[: k + 1]) for k in range(4)]
+    back = [entered(4 + k, both[: 5 + k]) for k in range(4)]
     count = ay_ref.shape[0] // 8
     load = lambda ref: lambda i: ref[8 * i : 8 * i + 8, :]
     load_a = load(ay_ref)
@@ -192,10 +220,8 @@
     def keep(i, value):
         z_ref[8 * i : 8 * i + 8, :] = value
 
-    start = [s_ref[mine, k] for k in range(4)]
-    sweep(count, start, load(wide_ref), load_a, gain, keep, False)
-    start = [t_ref[mine, k] for k in range(4)]
-    sweep(count, start, load(z_ref), load_a, gain, keep, True)
+    sweep(count, ahead, load(wide_ref), load_a, gain, keep, False)
+    sweep(count, back, load(z_ref), load_a, gain, keep, True)
     for tile in range(3):
         turned = z_ref[tile * LANES : (tile + 1) * LANES, :].T
         field_ref[:, tile * LANES : (tile + 1) * LANES] = turned[:half]
@@ -205,29 +231,31 @@
     whole = pl.BlockSpec(memory_space=VMEM)
     return pl.pallas_call(
         kernel,
-        out_shape=[jax.ShapeDtypeStruct(shape, F32) for shape in outs],
+        out_shape=[VMEM(shape, F32) for shape in outs],
         in_specs=[whole] * len(args),
         out_specs=[whole] * len(outs),
         scratch_shapes=[pltpu.VMEM(shape, F32) for shape in scratch],
-    )(*args)
+        compiler_params=pltpu.CompilerParams(vmem_limit_bytes=16 << 20),
+    )(*(pltpu.with_memory_space_constraint(a, VMEM) for a in args))
 
 
 def body(field, decay_x, decay_y):
     along_x, along_y = (lax.axis_size("gx"), lax.axis_size("gy"))
+    blocks = 8
+    rows_y = along_y // blocks
     rows, columns = field.shape
-    count = decay_y.shape[0]
     sent, grid, ax = call(
         x_ends,
         [(along_x, 32, LANES), (rows, 4, LANES), (rows, LANES)],
         [(32, LANES), (rows, 4, LANES)],
         field,
-        decay_x,
+        decay_x.T,
     )
     got = lax.all_to_all(sent, "gx", 0, 0, tiled=True)
-    (ay,) = call(y_decays, [(columns, LANES)], [], decay_y)
+    (ay,) = call(y_decays, [(columns, LANES)], [], decay_y.T)
     sent, wide = call(
         x_apply_y_ends,
-        [(along_y, 5, 8, LANES), (columns, LANES)],
+        [(blocks, 5, 8, LANES), (columns, LANES)],
         [
             (5, along_x * 8, LANES),
             (along_x, 4, 4, LANES),
@@ -240,12 +268,22 @@
         ax,
         ay,
     )
-    got = lax.all_to_all(sent, "gy", 0, 0, tiled=True)
+    near = [[blocks * r + k for k in range(blocks)] for r in range(rows_y)]
+    got = lax.all_to_all(sent, "gy", 0, 0, tiled=True, axis_index_groups=near)
+    sent, own = call(
+        y_join,
+        [(rows_y, 5, 8, LANES), (8, 8, LANES)],
+        [(blocks, 4, 8, LANES), (blocks, 4, 8, LANES)],
+        got,
+    )
+    far = [[blocks * r + k for r in range(rows_y)] for k in range(blocks)]
+    got = lax.all_to_all(sent, "gy", 0, 0, tiled=True, axis_index_groups=far)
     (out,) = call(
-        y_apply,
+        functools.partial(y_apply, blocks=blocks),
         [(rows, columns)],
-        [(along_y, 4, 8, LANES), (along_y, 4, 8, LANES), (columns, LANES)],
+        [(rows_y, 4, 8, LANES), (rows_y, 4, 8, LANES), (columns, LANES)],
         got,
+        own,
         wide,
         ay,
     )

time: 64.4 us -> 54.6 us (0.85)
  the two profiles are of different devices: /device:TPU:8 before, /device:TPU:1 now
where the time goes in v2:
time: 54.6 us; the launch traced here: 54.2 us
  blocking collectives  25.3 us (46%)
  starting transfers between devices  12 us (22%)
  waiting for transfers between devices  11.4 us (21%)
  Pallas kernels  3.29 us (6%)
  local copies, waits for them, and re-layouts  2.24 us (4%)
    all_to_all x1, blocking collectives, body(): got = lax.all_to_all(sent, 'gy', 0, 0, tiled=True, axis_index_groups=near)  16.9 us
    all_to_all x1, starting transfers between devices, body(): got = lax.all_to_all(sent, 'gx', 0, 0, tiled=True)  12 us
    all_to_all x1, waiting for transfers between devices, body(): got = lax.all_to_all(sent, 'gx', 0, 0, tiled=True)  11.4 us
    all_to_all x1, blocking collectives, body(): got = lax.all_to_all(sent, 'gy', 0, 0, tiled=True, axis_index_groups=far)  8.38 us
    pallas_call x5, Pallas kernels, call(): pl.pallas_call(kernel, out_shape=[VMEM(shape, F32) for shape in outs], in...  3.29 us
    unnamed x7, local copies, waits for them, and re-layouts  2.24 us
  transfers between devices with their start and end apart: 1, of which 1 were waited for; matrix products, arithmetic and copies ran while one was open for 0% of the time, Pallas kernels for 0%

profile of v2, /device:TPU:1, one launch (start us, length us, event | category | flops | bytes accessed | tf_op | source)
XLA Modules:
  0.0 54.2 jit_solution(14560100652779850735)
XLA Ops:
  0.0 0.0 copy-start
  0.0 0.9 %copy-done = f32[64,384]{1,0:T(8,128)S(1)} copy-done((f32[64,384]{1,0:T(8,128)S(1)}, f32[64,384]{1,0:T(8,128)}, u32[]{:S(2)}) %copy-start) | copy-done | bytes 98328
  0.9 0.0 copy-start.1
  0.9 0.7 %copy-done.1 = f32[64,8]{0,1:T(8,128)S(1)} copy-done((f32[64,8]{0,1:T(8,128)S(1)}, f32[64,8]{0,1:T(8,128)}, u32[]{:S(2)}) %copy-start.1) | copy-done | bytes 2072
  1.6 1.1 %shard_map.37 = (f32[16,32,128]{2,1,0:T(8,128)}, f32[64,4,128]{2,1,0:T(4,128)S(1)}, f32[64,128]{1,0:T(8,128)S(1)}) custom-call(f32[64,384]{1,0:T(8,128)S(1)} %copy-done, f32[8,64]{1,0:T(8,128)S(1)} %bitcast.4), custom_call_target="tpu_custom_call" | custom-call | tf_op jit(solution)/shard_map/pallas_call | solution.py:232
  2.7 0.0 copy-start.2
  2.7 12.0 %all-to-all-start = ((f32[16,32,128]{2,1,0:T(8,128)}), f32[16,32,128]{2,1,0:T(8,128)S(1)}, u32[]{:S(2)}, u32[]{:S(2)}) async-start(f32[16,32,128]{2,1,0:T(8,128)} %get-tuple-element.12), calls=%async_computation | async-start | bytes 524288 | tf_op jit(solution)/shard_map/all_to_all | solution.py:254
  14.7 0.0 copy-done.2
  14.7 0.1 shard_map.38.ay_ref
  14.8 11.4 %all-to-all-done = f32[16,32,128]{2,1,0:T(8,128)S(1)} async-done(((f32[16,32,128]{2,1,0:T(8,128)}), f32[16,32,128]{2,1,0:T(8,128)S(1)}, u32[]{:S(2)}, u32[]{:S(2)}) %all-to-all-start) | async-done | bytes 262176 | tf_op jit(solution)/shard_map/all_to_all | solution.py:254
  26.3 1.0 %shard_map.39 = (f32[8,5,8,128]{3,2,1,0:T(8,128)S(1)}, f32[384,128]{1,0:T(8,128)S(1)}) custom-call(f32[512,128]{1,0:T(8,128)S(1)} %bitcast.3, f32[64,4,128]{2,1,0:T(4,128)S(1)} %get-tuple-element.13.grid_ref, f32[64,128]{1,0:T(8,128)S(1)} %get-tuple-element.14.ax_ref, f32[384,128]{1,0:T(8,128)S(1)} %shard_map.38.ay_ref), custom_call_target="tpu_custom_call" | custom-call | tf_op jit(solution)/shard_map/pallas_call | solution.py:232
  27.3 16.9 %all_to_all.15.got_ref = f32[8,5,8,128]{3,2,1,0:T(8,128)S(1)} all-to-all(f32[8,5,8,128]{3,2,1,0:T(8,128)S(1)} %get-tuple-element.15), channel_id=1, replica_groups={{0,1,2,3,4,5,6,7},{8,9,10,11,12,13,14,15},{16,17,18,19,20,21,22,23},{24..., dimensions={0} | all-to-all | bytes 327680 | tf_op jit(solution)/shard_map/all_to_all | solution.py:272
  44.2 0.5 shard_map.40
  44.7 8.4 %all_to_all.16.got_ref = f32[4,5,8,128]{3,2,1,0:T(8,128)S(1)} all-to-all(f32[4,5,8,128]{3,2,1,0:T(8,128)S(1)} %get-tuple-element.16), channel_id=1, replica_groups={{0,8,16,24},{1,9,17,25},{2,10,18,26},{3,11,19,27},{4,12,20,28},{5,13,21..., dimensions={0} | all-to-all | bytes 163840 | tf_op jit(solution)/shard_map/all_to_all | solution.py:280
  53.1 0.5 shard_map.41
  53.6 0.7 %copy.4 = f32[64,384]{1,0:T(8,128)} copy(f32[64,384]{1,0:T(8,128)S(1)} %shard_map.41) | data formatting | bytes 196608
Async XLA Ops:
  0.0 0.9 %copy-start = (f32[64,384]{1,0:T(8,128)S(1)}, f32[64,384]{1,0:T(8,128)}, u32[]{:S(2)}) copy-start(f32[64,384]{1,0:T(8,128)} %field_ref.1) | copy-start | bytes 294916
  0.9 0.7 %copy-start.1 = (f32[64,8]{0,1:T(8,128)S(1)}, f32[64,8]{0,1:T(8,128)}, u32[]{:S(2)}) copy-start(f32[64,8]{0,1:T(8,128)} %param.4) | copy-start | bytes 6148
  2.7 12.0 %copy-start.2 = (f32[48,8]{0,1:T(8,128)S(1)}, f32[48,8]{0,1:T(8,128)}, u32[]{:S(2)}) copy-start(f32[48,8]{0,1:T(8,128)} %param.5) | copy-start | bytes 4612
  2.7 23.5 %all-to-all-start = ((f32[16,32,128]{2,1,0:T(8,128)}), f32[16,32,128]{2,1,0:T(8,128)S(1)}, u32[]{:S(2)}, u32[]{:S(2)}) async-start(f32[16,32,128]{2,1,0:T(8,128)} %get-tuple-element.12), calls=%async_computation | async-start | bytes 524288 | tf_op jit(solution)/shard_map/all_to_all | solution.py:254

commit v3 on v2

v3 whole, which is shorter than its diff:
```python
import functools

import jax
import jax.numpy as jnp
from jax import lax
from jax.experimental import pallas as pl
from jax.experimental.pallas import tpu as pltpu
from jax.sharding import PartitionSpec as P

F32 = jnp.float32
LANES = 128
VMEM, HBM = (pltpu.MemorySpace.VMEM, pltpu.MemorySpace.HBM)


def iota(shape, dim):
    return lax.broadcasted_iota(jnp.int32, shape, dim)


def take_lanes(values, lanes):
    return jnp.take_along_axis(values, jnp.broadcast_to(lanes, values.shape), axis=1)


def cascade(states, value, decay, gain):
    moved = []
    for state in states:
        value = decay * state + gain * value
        moved.append(value)
    return moved


def toeplitz(column, states):
    return [
        sum((column[row - k] * states[k] for k in range(1, row + 1)), column[row] * states[0])
        for row in range(4)
    ]


def sweep(steps, states, load, decay, gain, store, reverse):
    for step in reversed(range(steps)) if reverse else range(steps):
        states = cascade(states, load(step), decay(step), gain(step))
        if store is not None:
            store(step, states[3])
    return states


def x_ends(
    field_ref, decay_ref, sent_ref, grid_ref, a_ref, near_ref, short_ref, wide_ref, out_ref, sems
):
    levels, steps = decay_ref.shape
    tiles = field_ref.shape[1] // LANES
    copies = [
        pltpu.make_async_copy(decay_ref, short_ref, sems.at[0]),
        pltpu.make_async_copy(field_ref, near_ref, sems.at[1]),
    ]
    for copy in copies:
        copy.start()
    copies[0].wait()
    periodic = jnp.concatenate([short_ref[...]] * (LANES // levels), axis=0).T
    for row in range(4):
        a_ref[:, row, :] = periodic
    grid_ref[:, tiles, :] = jnp.zeros((steps, LANES), F32)
    copies[1].wait()
    for tile in range(tiles):
        grid_ref[:, tile, :] = near_ref[:, tile * LANES : (tile + 1) * LANES]
    row, lane = (iota((4, LANES), 0), iota((4, LANES), 1))
    unit = [((row == tiles) & (lane // levels == k)).astype(F32) for k in range(8)]
    chunk = 16

    def ahead_steps(c, states):
        for step in range(chunk):
            i = c * chunk + step
            a = a_ref[i]
            states = cascade(states, grid_ref[i], a, 1.0 - a)
            out_ref[i] = states[3]
        return tuple(states)

    def back_steps(c, states):
        for step in range(chunk):
            i = steps - 1 - c * chunk - step
            a = a_ref[i]
            states = cascade(states, out_ref[i], a, 1.0 - a)
        return tuple(states)

    ahead = lax.fori_loop(0, steps // chunk, ahead_steps, tuple(unit[:4]))
    back = lax.fori_loop(0, steps // chunk, back_steps, tuple(unit[4:]))
    for k, end in enumerate(ahead + back):
        wide_ref[tiles * k : tiles * (k + 1), :] = end[:tiles]
    first = second = jnp.zeros((4, LANES), F32)
    for k in range(4):
        first += pltpu.roll(jnp.where(lane < 32, back[k], 0.0), 32 * k, 1)
        second += pltpu.roll(jnp.where(lane < 8, ahead[k], 0.0), 16 * k, 1)
        own = jnp.where((lane >= 32) & (lane < 40), back[k], 0.0)
        second += pltpu.roll(own, (16 * k - 24) % LANES, 1)
    wide_ref[24:25, :] = first[tiles:]
    wide_ref[25:26, :] = second[tiles:]
    wide_ref[26:32, :] = jnp.zeros((6, LANES), F32)
    for part in range(sent_ref.shape[1]):
        rows = wide_ref[4 * part : 4 * part + 4, :]
        for device in range(sent_ref.shape[0]):
            sent_ref[device, part] = rows


def y_decays(decay_ref, a_ref):
    decays = decay_ref[...]
    for step in range(decays.shape[1]):
        a_ref[8 * step : 8 * step + 8, :] = lane_of(decays, step)


def lane_of(values, at):
    return jnp.broadcast_to(values[:, at : at + 1], (8, LANES))


def pack(ahead, back, lane):
    half = LANES // 2
    tiles = [jnp.where(lane < half, ahead[k], pltpu.roll(back[k], half, 1)) for k in range(4)]
    packed = jnp.zeros((8, LANES), F32)
    for k in range(4):
        for shift, ends in ((0, back), (8, ahead)):
            at = 16 * k + shift
            moved = pltpu.roll(ends[k], (at - half) % LANES, 1)
            packed = jnp.where((lane >= at) & (lane < at + 8), moved, packed)
    return [*tiles, packed]


def chained(got_ref, head, ahead, back, s_ref, t_ref):
    blocks, half = (got_ref.shape[0], LANES // 2)
    low = iota((8, LANES), 1) < half
    for m in range(blocks):
        at = (m - head) % blocks
        packed = got_ref[at, 4]
        for k in range(4):
            s_ref[m, k] = ahead[k]
        moved = toeplitz([lane_of(packed, 16 * k + 8) for k in range(4)], ahead)
        ahead = [moved[k] + jnp.where(low, got_ref[at, k], 0.0) for k in range(4)]
    for m in reversed(range(blocks)):
        at = (m - head) % blocks
        packed = got_ref[at, 4]
        for k in range(4):
            t_ref[m, k] = back[k]
        moved = toeplitz([lane_of(packed, 16 * k + 4) for k in range(4)], back)
        turned = [
            sum(lane_of(packed, 16 * r + k) * s_ref[m, k] for k in range(4))
            + jnp.where(low, pltpu.roll(got_ref[at, r], half, 1), 0.0)
            for r in range(4)
        ]
        back = [moved[k] + turned[k] for k in range(4)]
    return ahead, back


def x_apply_y_ends(
    got_ref,
    grid_ref,
    ax_ref,
    ay_ref,
    sent_ref,
    wide_ref,
    maps_ref,
    s_ref,
    t_ref,
    z_ref,
    out_ref,
    *,
    head,
):
    steps = grid_ref.shape[0]
    devices, rows = (s_ref.shape[0], 28)
    mine = lax.axis_index("gx")
    first, second = (got_ref[pl.ds(24 + k, devices, stride=rows), :] for k in range(2))
    lane = iota(first.shape, 1) % 8
    for k in range(4):
        for start in range(4):
            maps_ref[4 * k + start] = take_lanes(first, lane + 32 * k + 8 * start)
        maps_ref[16 + k] = take_lanes(second, lane + 16 * k)
        maps_ref[20 + k] = take_lanes(second, lane + 16 * k + 8)

    def end(m, k):
        start = rows * ((m - head) % devices) + 3 * k
        return got_ref[start : start + 4, :]

    def entry(at, m):
        slot = (m - head) % devices
        return maps_ref[at, slot : slot + 1, :]

    zero = jnp.zeros((4, LANES), F32)
    states = [zero] * 4
    for m in range(devices):
        for k in range(4):
            s_ref[m, k] = states[k]
        if m < devices - 1:
            moved = toeplitz([entry(16 + k, m) for k in range(4)], states)
            states = [moved[k] + end(m, k) for k in range(4)]
    states = [zero] * 4
    for m in reversed(range(devices)):
        for k in range(4):
            t_ref[m, k] = states[k]
        if m > 0:
            moved = toeplitz([entry(20 + k, m) for k in range(4)], states)
            turned = [
                sum(entry(4 * r + k, m) * s_ref[m, k] for k in range(4)) + end(m, 4 + r)
                for r in range(4)
            ]
            states = [moved[k] + turned[k] for k in range(4)]
    load_a = lambda i: ax_ref[i]
    gain = lambda i: 1.0 - ax_ref[i]

    def keep(i, value):
        z_ref[i] = value

    start = [s_ref[mine, k] for k in range(4)]
    sweep(steps, start, lambda i: grid_ref[i], load_a, gain, keep, False)
    start = [t_ref[mine, k] for k in range(4)]
    sweep(steps, start, lambda i: z_ref[i], load_a, gain, keep, True)
    wide_ref[...] = jnp.zeros(wide_ref.shape, F32)
    for tile in range(3):
        wide_ref[tile * LANES : (tile + 1) * LANES, :steps] = z_ref[:, tile, :].T

    lane = iota((8, LANES), 1)
    unit = [(lane == steps + k).astype(F32) for k in range(8)]
    count = ay_ref.shape[0] // 8
    load = lambda ref: lambda i: ref[8 * i : 8 * i + 8, :]
    load_a = load(ay_ref)
    gain = lambda i: 1.0 - load_a(i)

    def keep_y(i, value):
        out_ref[8 * i : 8 * i + 8, :] = value

    ahead = sweep(count, unit[:4], load(wide_ref), load_a, gain, keep_y, False)
    back = sweep(count, unit[4:], load(out_ref), load_a, gain, None, True)
    tiles = pack(ahead, back, lane)
    for device in range(sent_ref.shape[0]):
        for k in range(5):
            sent_ref[device, k] = tiles[k]


def y_join(got_ref, sent_ref, mine_ref, s_ref, t_ref, *, head):
    blocks = got_ref.shape[0]
    lane = iota((8, LANES), 1)
    unit = [(lane == LANES // 2 + k).astype(F32) for k in range(8)]
    ahead, back = chained(got_ref, head, unit[:4], unit[4:], s_ref, t_ref)
    tiles = pack(ahead, back, lane)
    for device in range(sent_ref.shape[0]):
        for k in range(5):
            sent_ref[device, k] = tiles[k]
    mine = lax.axis_index("gy") % blocks
    for k in range(4):
        mine_ref[k] = s_ref[mine, k]
        mine_ref[4 + k] = t_ref[mine, k]


def y_apply(
    got_ref,
    mine_ref,
    wide_ref,
    ay_ref,
    field_ref,
    s_ref,
    t_ref,
    z_ref,
    done_ref,
    sems,
    *,
    blocks,
    head,
):
    half = LANES // 2
    zero = [jnp.zeros((8, LANES), F32)] * 4
    chained(got_ref, head, zero, zero, s_ref, t_ref)
    mine = lax.axis_index("gy") // blocks
    ahead = [s_ref[mine, k] for k in range(4)]
    back = [t_ref[mine, k] for k in range(4)]

    def entered(k, starts):
        found = mine_ref[k]
        return found + sum(lane_of(found, half + at) * state for at, state in starts)

    first = [(k, ahead[k]) for k in range(4)]
    both = first + [(4 + k, back[k]) for k in range(4)]
    ahead = [entered(k, first[: k + 1]) for k in range(4)]
    back = [entered(4 + k, both[: 5 + k]) for k in range(4)]
    count = ay_ref.shape[0] // 8
    load = lambda ref: lambda i: ref[8 * i : 8 * i + 8, :]
    load_a = load(ay_ref)
    gain = lambda i: 1.0 - load_a(i)

    def keep(i, value):
        z_ref[8 * i : 8 * i + 8, :] = value

    sweep(count, ahead, load(wide_ref), load_a, gain, keep, False)
    copies, part = ([], LANES // 8)
    for tile in reversed(range(3)):
        shifted = lambda get: lambda i: get(tile * part + i)
        put = lambda i, value: keep(tile * part + i, value)
        back = sweep(part, back, shifted(load(z_ref)), shifted(load_a), shifted(gain), put, True)
        done_ref[tile] = z_ref[tile * LANES : (tile + 1) * LANES, :].T[:half]
        to = field_ref.at[:, tile * LANES : (tile + 1) * LANES]
        copies.append(pltpu.make_async_copy(done_ref.at[tile], to, sems.at[tile]))
        copies[-1].start()
    for copy in copies:
        copy.wait()


def call(kernel, outs, scratch, *args, away_in=0, away_out=0, sems=0):
    here, away = (pl.BlockSpec(memory_space=space) for space in (VMEM, HBM))
    scratch = [pltpu.VMEM(shape, F32) for shape in scratch]
    return pl.pallas_call(
        kernel,
        out_shape=[jax.ShapeDtypeStruct(shape, F32) for shape in outs[:away_out]]
        + [VMEM(shape, F32) for shape in outs[away_out:]],
        in_specs=[away] * away_in + [here] * (len(args) - away_in),
        out_specs=[away] * away_out + [here] * (len(outs) - away_out),
        scratch_shapes=scratch + [pltpu.SemaphoreType.DMA((sems,))] * (sems > 0),
        compiler_params=pltpu.CompilerParams(vmem_limit_bytes=16 << 20),
    )(*(pltpu.with_memory_space_constraint(a, HBM if k < away_in else VMEM) for k, a in enumerate(args)))


def exchange(sent, axis, groups, head):
    groups = [group[head:] + group[:head] for group in groups]
    return lax.all_to_all(sent, axis, 0, 0, tiled=True, axis_index_groups=groups)


def body(field, decay_x, decay_y):
    along_x, along_y = (lax.axis_size("gx"), lax.axis_size("gy"))
    blocks = 8
    rows_y = along_y // blocks
    head_x, head_near, head_far = (along_x * 3 // 4, blocks // 2, rows_y // 2)
    rows, columns = field.shape
    sent, grid, ax = call(
        x_ends,
        [(along_x, 7, 4, LANES), (rows, 4, LANES), (rows, 4, LANES)],
        [(rows, columns), decay_x.T.shape, (32, LANES), (rows, 4, LANES)],
        field,
        decay_x.T,
        away_in=2,
        sems=2,
    )
    got = exchange(sent, "gx", [list(range(along_x))], head_x)
    (ay,) = call(y_decays, [(columns, LANES)], [], decay_y.T)
    sent, wide = call(
        functools.partial(x_apply_y_ends, head=head_x),
        [(blocks, 5, 8, LANES), (columns, LANES)],
        [
            (24, along_x, LANES),
            (along_x, 4, 4, LANES),
            (along_x, 4, 4, LANES),
            (rows, 4, LANES),
            (columns, LANES),
        ],
        got.reshape(along_x * 28, LANES),
        grid,
        ax,
        ay,
    )
    near = [[blocks * r + k for k in range(blocks)] for r in range(rows_y)]
    got = exchange(sent, "gy", near, head_near)
    sent, own = call(
        functools.partial(y_join, head=head_near),
        [(rows_y, 5, 8, LANES), (8, 8, LANES)],
        [(blocks, 4, 8, LANES), (blocks, 4, 8, LANES)],
        got,
    )
    far = [[blocks * r + k for r in range(rows_y)] for k in range(blocks)]
    got = exchange(sent, "gy", far, head_far)
    (out,) = call(
        functools.partial(y_apply, blocks=blocks, head=head_far),
        [(rows, columns)],
        [(rows_y, 4, 8, LANES), (rows_y, 4, 8, LANES), (columns, LANES), (3, rows, LANES)],
        got,
        own,
        wide,
        ay,
        away_out=1,
        sems=3,
    )
    return out


def solution(mesh):
    placed = (P("gx", "gy"), P("gx", None), P("gy", None))
    return jax.shard_map(body, mesh=mesh, in_specs=placed, out_specs=P("gx", "gy"), check_vma=False)
```

time: 54.6 us -> 46.6 us (0.85)
  the two profiles are of different devices: /device:TPU:1 before, /device:TPU:4 now
where the time goes in v3:
time: 46.6 us; the launch traced here: 46.3 us
  blocking collectives  21.3 us (46%)
  starting transfers between devices  12.4 us (27%)
  waiting for transfers between devices  7.64 us (16%)
  Pallas kernels  4.89 us (10%)
    all_to_all x2, blocking collectives, exchange(): lax.all_to_all(sent, axis, 0, 0, tiled=True, axis_index_groups=groups)  21.3 us
    all_to_all x1, starting transfers between devices, exchange(): lax.all_to_all(sent, axis, 0, 0, tiled=True, axis_index_groups=groups)  12.4 us
    all_to_all x1, waiting for transfers between devices, exchange(): lax.all_to_all(sent, axis, 0, 0, tiled=True, axis_index_groups=groups)  7.64 us
    pallas_call x5, Pallas kernels, call(): pl.pallas_call(kernel, out_shape=[jax.ShapeDtypeStruct(shape, F32) for sh...  4.89 us
  transfers between devices with their start and end apart: 1, of which 1 were waited for; matrix products, arithmetic and copies ran while one was open for 0% of the time, Pallas kernels for 0%

profile of v3, /device:TPU:4, one launch (start us, length us, event | category | flops | bytes accessed | tf_op | source)
XLA Modules:
  0.0 46.3 jit_solution(17765652931971363963)
XLA Ops:
  0.0 2.1 %shard_map.37 = (f32[16,7,4,128]{3,2,1,0:T(4,128)}, f32[64,4,128]{2,1,0:T(4,128)S(1)}, f32[64,4,128]{2,1,0:T(4,128)S(1)}) custom-call(f32[64,384]{1,0:T(8,128)} %field_ref.1, f32[8,64]{1,0:T(8,128)} %bitcast.5), custom_call_target="tpu_custom_call" | custom-call | tf_op jit(solution)/shard_map/pallas_call | solution.py:305
  2.1 0.0 copy-start
  2.2 12.4 %all-to-all-start = ((f32[16,7,4,128]{3,2,1,0:T(4,128)}), f32[16,7,4,128]{3,2,1,0:T(4,128)S(1)}, u32[]{:S(2)}, u32[]{:S(2)}) async-start(f32[16,7,4,128]{3,2,1,0:T(4,128)} %get-tuple-element.12), calls=%async_computation | async-start | bytes 458752 | tf_op jit(solution)/shard_map/all_to_all | solution.py:318
  14.5 0.0 copy-done
  14.5 0.1 shard_map.38.ay_ref
  14.7 7.6 %all-to-all-done = f32[16,7,4,128]{3,2,1,0:T(4,128)S(1)} async-done(((f32[16,7,4,128]{3,2,1,0:T(4,128)}), f32[16,7,4,128]{3,2,1,0:T(4,128)S(1)}, u32[]{:S(2)}, u32[]{:S(2)}) %all-to-all-start) | async-done | bytes 229408 | tf_op jit(solution)/shard_map/all_to_all | solution.py:318
  22.3 1.0 %shard_map.39 = (f32[8,5,8,128]{3,2,1,0:T(8,128)S(1)}, f32[384,128]{1,0:T(8,128)S(1)}) custom-call(f32[448,128]{1,0:T(8,128)S(1)} %bitcast.3, f32[64,4,128]{2,1,0:T(4,128)S(1)} %get-tuple-element.13.grid_ref, f32[64,4,128]{2,1,0:T(4,128)S(1)} %get-tuple-element.14.ax_ref, f32[384,128]{1,0:T(8,128)S(1)} %shard_map.38.ay_ref), custom_call_target="tpu_custom_call" | custom-call | tf_op jit(solution)/shard_map/pallas_call | solution.py:305
  23.3 13.2 %all_to_all.15.got_ref = f32[8,5,8,128]{3,2,1,0:T(8,128)S(1)} all-to-all(f32[8,5,8,128]{3,2,1,0:T(8,128)S(1)} %get-tuple-element.15), channel_id=1, replica_groups={{4,5,6,7,0,1,2,3},{12,13,14,15,8,9,10,11},{20,21,22,23,16,17,18,19},{28..., dimensions={0} | all-to-all | bytes 327680 | tf_op jit(solution)/shard_map/all_to_all | solution.py:318
  36.6 0.5 %shard_map.40 = (f32[4,5,8,128]{3,2,1,0:T(8,128)S(1)}, f32[8,8,128]{2,1,0:T(8,128)S(1)}) custom-call(f32[8,5,8,128]{3,2,1,0:T(8,128)S(1)} %all_to_all.15.got_ref), custom_call_target="tpu_custom_call" | custom-call | tf_op jit(solution)/shard_map/pallas_call | solution.py:305
  37.1 8.1 %all_to_all.16.got_ref = f32[4,5,8,128]{3,2,1,0:T(8,128)S(1)} all-to-all(f32[4,5,8,128]{3,2,1,0:T(8,128)S(1)} %get-tuple-element.16), channel_id=1, replica_groups={{16,24,0,8},{17,25,1,9},{18,26,2,10},{19,27,3,11},{20,28,4,12},{21,29,5..., dimensions={0} | all-to-all | bytes 163840 | tf_op jit(solution)/shard_map/all_to_all | solution.py:318
  45.2 1.1 %shard_map.41 = f32[64,384]{1,0:T(8,128)} custom-call(f32[4,5,8,128]{3,2,1,0:T(8,128)S(1)} %all_to_all.16.got_ref, f32[8,8,128]{2,1,0:T(8,128)S(1)} %get-tuple-element.17.mine_ref, f32[384,128]{1,0:T(8,128)S(1)} %get-tuple-element.18.wide_ref, f32[384,128]{1,0:T(8,128)S(1)} %shard_map.38.ay_ref), custom_call_target="tpu_custom_call" | custom-call | tf_op jit(solution)/shard_map/pallas_call | solution.py:305
Async XLA Ops:
  2.1 12.4 %copy-start = (f32[48,8]{0,1:T(8,128)S(1)}, f32[48,8]{0,1:T(8,128)}, u32[]{:S(2)}) copy-start(f32[48,8]{0,1:T(8,128)} %param.5) | copy-start | bytes 4612
  2.2 20.2 %all-to-all-start = ((f32[16,7,4,128]{3,2,1,0:T(4,128)}), f32[16,7,4,128]{3,2,1,0:T(4,128)S(1)}, u32[]{:S(2)}, u32[]{:S(2)}) async-start(f32[16,7,4,128]{3,2,1,0:T(4,128)} %get-tuple-element.12), calls=%async_computation | async-start | bytes 458752 | tf_op jit(solution)/shard_map/all_to_all | solution.py:318

commit v4 on v3

--- a/solution.py
+++ b/solution.py
@@ -44,13 +44,26 @@
 
 
 def x_ends(
-    field_ref, decay_ref, sent_ref, grid_ref, a_ref, near_ref, short_ref, wide_ref, out_ref, sems
+    field_ref,
+    decay_ref,
+    other_ref,
+    sent_ref,
+    grid_ref,
+    a_ref,
+    ay_ref,
+    near_ref,
+    short_ref,
+    turned_ref,
+    wide_ref,
+    out_ref,
+    sems,
 ):
     levels, steps = decay_ref.shape
     tiles = field_ref.shape[1] // LANES
     copies = [
         pltpu.make_async_copy(decay_ref, short_ref, sems.at[0]),
-        pltpu.make_async_copy(field_ref, near_ref, sems.at[1]),
+        pltpu.make_async_copy(other_ref, turned_ref, sems.at[1]),
+        pltpu.make_async_copy(field_ref, near_ref, sems.at[2]),
     ]
     for copy in copies:
         copy.start()
@@ -60,6 +73,8 @@
         a_ref[:, row, :] = periodic
     grid_ref[:, tiles, :] = jnp.zeros((steps, LANES), F32)
     copies[1].wait()
+    y_decays(turned_ref, ay_ref)
+    copies[2].wait()
     for tile in range(tiles):
         grid_ref[:, tile, :] = near_ref[:, tile * LANES : (tile + 1) * LANES]
     row, lane = (iota((4, LANES), 0), iota((4, LANES), 1))
@@ -122,18 +137,18 @@
     return [*tiles, packed]
 
 
-def chained(got_ref, head, ahead, back, s_ref, t_ref):
+def chained(got_ref, order, ahead, back, s_ref, t_ref):
     blocks, half = (got_ref.shape[0], LANES // 2)
     low = iota((8, LANES), 1) < half
     for m in range(blocks):
-        at = (m - head) % blocks
+        at = order.index(m)
         packed = got_ref[at, 4]
         for k in range(4):
             s_ref[m, k] = ahead[k]
         moved = toeplitz([lane_of(packed, 16 * k + 8) for k in range(4)], ahead)
         ahead = [moved[k] + jnp.where(low, got_ref[at, k], 0.0) for k in range(4)]
     for m in reversed(range(blocks)):
-        at = (m - head) % blocks
+        at = order.index(m)
         packed = got_ref[at, 4]
         for k in range(4):
             t_ref[m, k] = back[k]
@@ -160,7 +175,7 @@
     z_ref,
     out_ref,
     *,
-    head,
+    order,
 ):
     steps = grid_ref.shape[0]
     devices, rows = (s_ref.shape[0], 28)
@@ -174,11 +189,11 @@
         maps_ref[20 + k] = take_lanes(second, lane + 16 * k + 8)
 
     def end(m, k):
-        start = rows * ((m - head) % devices) + 3 * k
+        start = rows * order.index(m) + 3 * k
         return got_ref[start : start + 4, :]
 
     def entry(at, m):
-        slot = (m - head) % devices
+        slot = order.index(m)
         return maps_ref[at, slot : slot + 1, :]
 
     zero = jnp.zeros((4, LANES), F32)
@@ -232,11 +247,11 @@
             sent_ref[device, k] = tiles[k]
 
 
-def y_join(got_ref, sent_ref, mine_ref, s_ref, t_ref, *, head):
+def y_join(got_ref, sent_ref, mine_ref, s_ref, t_ref, *, order):
     blocks = got_ref.shape[0]
     lane = iota((8, LANES), 1)
     unit = [(lane == LANES // 2 + k).astype(F32) for k in range(8)]
-    ahead, back = chained(got_ref, head, unit[:4], unit[4:], s_ref, t_ref)
+    ahead, back = chained(got_ref, order, unit[:4], unit[4:], s_ref, t_ref)
     tiles = pack(ahead, back, lane)
     for device in range(sent_ref.shape[0]):
         for k in range(5):
@@ -260,11 +275,11 @@
     sems,
     *,
     blocks,
-    head,
+    order,
 ):
     half = LANES // 2
     zero = [jnp.zeros((8, LANES), F32)] * 4
-    chained(got_ref, head, zero, zero, s_ref, t_ref)
+    chained(got_ref, order, zero, zero, s_ref, t_ref)
     mine = lax.axis_index("gy") // blocks
     ahead = [s_ref[mine, k] for k in range(4)]
     back = [t_ref[mine, k] for k in range(4)]
@@ -313,30 +328,40 @@
     )(*(pltpu.with_memory_space_constraint(a, HBM if k < away_in else VMEM) for k, a in enumerate(args)))
 
 
-def exchange(sent, axis, groups, head):
-    groups = [group[head:] + group[:head] for group in groups]
+def exchange(sent, axis, groups, order):
+    groups = [[group[k] for k in order] for group in groups]
     return lax.all_to_all(sent, axis, 0, 0, tiled=True, axis_index_groups=groups)
+
+
+def ring(members, head):
+    return [(head + k) % members for k in range(members)]
+
+
+def far_first(chips, head):
+    pairs = [(chip, core) for chip in ring(chips, head)[: chips // 2] for core in (1, 0)]
+    return [2 * ((chip + far) % chips) + core for chip, core in pairs for far in (0, chips // 2)]
 
 
 def body(field, decay_x, decay_y):
     along_x, along_y = (lax.axis_size("gx"), lax.axis_size("gy"))
     blocks = 8
     rows_y = along_y // blocks
-    head_x, head_near, head_far = (along_x * 3 // 4, blocks // 2, rows_y // 2)
+    order_x = far_first(along_x // 2, along_x * 3 // 8)
+    order_near, order_far = (ring(blocks, blocks // 2), ring(rows_y, rows_y // 2))
     rows, columns = field.shape
-    sent, grid, ax = call(
+    sent, grid, ax, ay = call(
         x_ends,
-        [(along_x, 7, 4, LANES), (rows, 4, LANES), (rows, 4, LANES)],
-        [(rows, columns), decay_x.T.shape, (32, LANES), (rows, 4, LANES)],
+        [(along_x, 7, 4, LANES), (rows, 4, LANES), (rows, 4, LANES), (columns, LANES)],
+        [(rows, columns), decay_x.T.shape, decay_y.T.shape, (32, LANES), (rows, 4, LANES)],
         field,
         decay_x.T,
-        away_in=2,
-        sems=2,
+        decay_y.T,
+        away_in=3,
+        sems=3,
     )
-    got = exchange(sent, "gx", [list(range(along_x))], head_x)
-    (ay,) = call(y_decays, [(columns, LANES)], [], decay_y.T)
+    got = exchange(sent, "gx", [list(range(along_x))], order_x)
     sent, wide = call(
-        functools.partial(x_apply_y_ends, head=head_x),
+        functools.partial(x_apply_y_ends, order=order_x),
         [(blocks, 5, 8, LANES), (columns, LANES)],
         [
             (24, along_x, LANES),
@@ -351,17 +376,17 @@
         ay,
     )
     near = [[blocks * r + k for k in range(blocks)] for r in range(rows_y)]
-    got = exchange(sent, "gy", near, head_near)
+    got = exchange(sent, "gy", near, order_near)
     sent, own = call(
-        functools.partial(y_join, head=head_near),
+        functools.partial(y_join, order=order_near),
         [(rows_y, 5, 8, LANES), (8, 8, LANES)],
         [(blocks, 4, 8, LANES), (blocks, 4, 8, LANES)],
         got,
     )
     far = [[blocks * r + k for r in range(rows_y)] for k in range(blocks)]
-    got = exchange(sent, "gy", far, head_far)
+    got = exchange(sent, "gy", far, order_far)
     (out,) = call(
-        functools.partial(y_apply, blocks=blocks, head=head_far),
+        functools.partial(y_apply, blocks=blocks, order=order_far),
         [(rows, columns)],
         [(rows_y, 4, 8, LANES), (rows_y, 4, 8, LANES), (columns, LANES), (3, rows, LANES)],
         got,

time: 46.6 us -> 43.3 us (0.929)
  blocking collectives: 21.3 us -> 38.9 us
  starting transfers between devices: 12.4 us -> 0 us
  waiting for transfers between devices: 7.64 us -> 0 us
  Pallas kernels: 4.89 us -> 4.14 us
    all_to_all x2 -> x3, blocking collectives: 21.3 us -> 38.9 us  [exchange(): lax.all_to_all(sent, axis, 0, 0, tiled=True, axis_index_groups=groups)]
    all_to_all x1 -> x0, starting transfers between devices: 12.4 us -> none  [exchange(): lax.all_to_all(sent, axis, 0, 0, tiled=True, axis_index_groups=groups)]
    all_to_all x1 -> x0, waiting for transfers between devices: 7.64 us -> none  [exchange(): lax.all_to_all(sent, axis, 0, 0, tiled=True, axis_index_groups=groups)]
    pallas_call x5 -> x4, Pallas kernels: 4.89 us -> 4.14 us  [call(): pl.pallas_call(kernel, out_shape=[jax.ShapeDtypeStruct(shape, F32) for sh...]
  transfers between devices with their start and end apart: 1 -> 0, of which waited for: 1 -> 0; matrix products, arithmetic and copies ran while one was open for 0% -> 0% of each run, Pallas kernels for 0% -> 0%
where the time goes in v4:
time: 43.3 us; the launch traced here: 43.1 us
  blocking collectives  38.9 us (90%)
  Pallas kernels  4.14 us (10%)
    all_to_all x3, blocking collectives, exchange(): lax.all_to_all(sent, axis, 0, 0, tiled=True, axis_index_groups=groups)  38.9 us
    pallas_call x4, Pallas kernels, call(): pl.pallas_call(kernel, out_shape=[jax.ShapeDtypeStruct(shape, F32) for sh...  4.14 us

profile of v4, /device:TPU:4, one launch (start us, length us, event | category | flops | bytes accessed | tf_op | source)
XLA Modules:
  0.0 43.1 jit_solution(399545725981635167)
XLA Ops:
  0.0 1.5 %shard_map.37 = (f32[16,7,4,128]{3,2,1,0:T(4,128)S(1)}, f32[64,4,128]{2,1,0:T(4,128)S(1)}, f32[64,4,128]{2,1,0:T(4,128)S(1)}, f32[384,128]{1,0:T(8,128)S(1)}) custom-call(f32[64,384]{1,0:T(8,128)} %field_ref.1, f32[8,64]{1,0:T(8,128)} %bitcast.4, f32[8,48]{1,0:T(8,128)} %bitcast.5), custom_call_target="tpu_custom_call" | custom-call | tf_op jit(solution)/shard_map/pallas_call | solution.py:320
  1.5 17.9 %all_to_all.15 = f32[16,7,4,128]{3,2,1,0:T(4,128)S(1)} all-to-all(f32[16,7,4,128]{3,2,1,0:T(4,128)S(1)} %get-tuple-element.13), channel_id=1, replica_groups={{416,160,384,128,480,224,448,192,32,288,0,256,96,352,64,320},{417,161,3..., dimensions={0} | all-to-all | bytes 458752 | tf_op jit(solution)/shard_map/all_to_all | solution.py:333
  19.5 1.0 %shard_map.38 = (f32[8,5,8,128]{3,2,1,0:T(8,128)S(1)}, f32[384,128]{1,0:T(8,128)S(1)}) custom-call(f32[448,128]{1,0:T(8,128)S(1)} %bitcast.3, f32[64,4,128]{2,1,0:T(4,128)S(1)} %get-tuple-element.14.grid_ref, f32[64,4,128]{2,1,0:T(4,128)S(1)} %get-tuple-element.15.ax_ref, f32[384,128]{1,0:T(8,128)S(1)} %get-tuple-element.16.ay_ref), custom_call_target="tpu_custom_call" | custom-call | tf_op jit(solution)/shard_map/pallas_call | solution.py:320
  20.5 12.9 %all_to_all.16.got_ref = f32[8,5,8,128]{3,2,1,0:T(8,128)S(1)} all-to-all(f32[8,5,8,128]{3,2,1,0:T(8,128)S(1)} %get-tuple-element.17), channel_id=1, replica_groups={{4,5,6,7,0,1,2,3},{12,13,14,15,8,9,10,11},{20,21,22,23,16,17,18,19},{28..., dimensions={0} | all-to-all | bytes 327680 | tf_op jit(solution)/shard_map/all_to_all | solution.py:333
  33.4 0.5 %shard_map.39 = (f32[4,5,8,128]{3,2,1,0:T(8,128)S(1)}, f32[8,8,128]{2,1,0:T(8,128)S(1)}) custom-call(f32[8,5,8,128]{3,2,1,0:T(8,128)S(1)} %all_to_all.16.got_ref), custom_call_target="tpu_custom_call" | custom-call | tf_op jit(solution)/shard_map/pallas_call | solution.py:320
  33.9 8.1 %all_to_all.17.got_ref = f32[4,5,8,128]{3,2,1,0:T(8,128)S(1)} all-to-all(f32[4,5,8,128]{3,2,1,0:T(8,128)S(1)} %get-tuple-element.18), channel_id=1, replica_groups={{16,24,0,8},{17,25,1,9},{18,26,2,10},{19,27,3,11},{20,28,4,12},{21,29,5..., dimensions={0} | all-to-all | bytes 163840 | tf_op jit(solution)/shard_map/all_to_all | solution.py:333
  42.0 1.1 %shard_map.40 = f32[64,384]{1,0:T(8,128)} custom-call(f32[4,5,8,128]{3,2,1,0:T(8,128)S(1)} %all_to_all.17.got_ref, f32[8,8,128]{2,1,0:T(8,128)S(1)} %get-tuple-element.19.mine_ref, f32[384,128]{1,0:T(8,128)S(1)} %get-tuple-element.20.wide_ref, f32[384,128]{1,0:T(8,128)S(1)} %get-tuple-element.16.ay_ref), custom_call_target="tpu_custom_call" | custom-call | tf_op jit(solution)/shard_map/pallas_call | solution.py:320

commit v5 on v4

--- a/solution.py
+++ b/solution.py
@@ -108,9 +108,8 @@
         second += pltpu.roll(own, (16 * k - 24) % LANES, 1)
     wide_ref[24:25, :] = first[tiles:]
     wide_ref[25:26, :] = second[tiles:]
-    wide_ref[26:32, :] = jnp.zeros((6, LANES), F32)
     for part in range(sent_ref.shape[1]):
-        rows = wide_ref[4 * part : 4 * part + 4, :]
+        rows = wide_ref[2 * part : 2 * part + 2, :]
         for device in range(sent_ref.shape[0]):
             sent_ref[device, part] = rows
 
@@ -134,28 +133,33 @@
             at = 16 * k + shift
             moved = pltpu.roll(ends[k], (at - half) % LANES, 1)
             packed = jnp.where((lane >= at) & (lane < at + 8), moved, packed)
-    return [*tiles, packed]
-
-
-def chained(got_ref, order, ahead, back, s_ref, t_ref):
+    folded = jnp.where(lane[:4] < half, packed[:4], pltpu.roll(packed, half, 1)[4:])
+    return [part for tile in tiles for part in (tile[:4], tile[4:])] + [folded]
+
+
+def chained(got_ref, order, ahead, back, s_ref, t_ref, open_ref):
     blocks, half = (got_ref.shape[0], LANES // 2)
     low = iota((8, LANES), 1) < half
+    for place in range(blocks):
+        for k in range(9):
+            open_ref[place, 4 * k : 4 * k + 4, :] = got_ref[place, k]
+        open_ref[place, 36:40, :] = pltpu.roll(got_ref[place, 8], half, 1)
     for m in range(blocks):
         at = order.index(m)
-        packed = got_ref[at, 4]
+        packed = open_ref[at, 32:40, :]
         for k in range(4):
             s_ref[m, k] = ahead[k]
         moved = toeplitz([lane_of(packed, 16 * k + 8) for k in range(4)], ahead)
-        ahead = [moved[k] + jnp.where(low, got_ref[at, k], 0.0) for k in range(4)]
+        ahead = [moved[k] + jnp.where(low, open_ref[at, 8 * k : 8 * k + 8, :], 0.0) for k in range(4)]
     for m in reversed(range(blocks)):
         at = order.index(m)
-        packed = got_ref[at, 4]
+        packed = open_ref[at, 32:40, :]
         for k in range(4):
             t_ref[m, k] = back[k]
         moved = toeplitz([lane_of(packed, 16 * k + 4) for k in range(4)], back)
         turned = [
             sum(lane_of(packed, 16 * r + k) * s_ref[m, k] for k in range(4))
-            + jnp.where(low, pltpu.roll(got_ref[at, r], half, 1), 0.0)
+            + jnp.where(low, pltpu.roll(open_ref[at, 8 * r : 8 * r + 8, :], half, 1), 0.0)
             for r in range(4)
         ]
         back = [moved[k] + turned[k] for k in range(4)]
@@ -178,7 +182,7 @@
     order,
 ):
     steps = grid_ref.shape[0]
-    devices, rows = (s_ref.shape[0], 28)
+    devices, rows = (s_ref.shape[0], 26)
     mine = lax.axis_index("gx")
     first, second = (got_ref[pl.ds(24 + k, devices, stride=rows), :] for k in range(2))
     lane = iota(first.shape, 1) % 8
@@ -243,18 +247,18 @@
     back = sweep(count, unit[4:], load(out_ref), load_a, gain, None, True)
     tiles = pack(ahead, back, lane)
     for device in range(sent_ref.shape[0]):
-        for k in range(5):
+        for k in range(9):
             sent_ref[device, k] = tiles[k]
 
 
-def y_join(got_ref, sent_ref, mine_ref, s_ref, t_ref, *, order):
+def y_join(got_ref, sent_ref, mine_ref, s_ref, t_ref, open_ref, *, order):
     blocks = got_ref.shape[0]
     lane = iota((8, LANES), 1)
     unit = [(lane == LANES // 2 + k).astype(F32) for k in range(8)]
-    ahead, back = chained(got_ref, order, unit[:4], unit[4:], s_ref, t_ref)
+    ahead, back = chained(got_ref, order, unit[:4], unit[4:], s_ref, t_ref, open_ref)
     tiles = pack(ahead, back, lane)
     for device in range(sent_ref.shape[0]):
-        for k in range(5):
+        for k in range(9):
             sent_ref[device, k] = tiles[k]
     mine = lax.axis_index("gy") % blocks
     for k in range(4):
@@ -270,6 +274,7 @@
     field_ref,
     s_ref,
     t_ref,
+    open_ref,
     z_ref,
     done_ref,
     sems,
@@ -279,7 +284,7 @@
 ):
     half = LANES // 2
     zero = [jnp.zeros((8, LANES), F32)] * 4
-    chained(got_ref, order, zero, zero, s_ref, t_ref)
+    chained(got_ref, order, zero, zero, s_ref, t_ref, open_ref)
     mine = lax.axis_index("gy") // blocks
     ahead = [s_ref[mine, k] for k in range(4)]
     back = [t_ref[mine, k] for k in range(4)]
@@ -351,7 +356,7 @@
     rows, columns = field.shape
     sent, grid, ax, ay = call(
         x_ends,
-        [(along_x, 7, 4, LANES), (rows, 4, LANES), (rows, 4, LANES), (columns, LANES)],
+        [(along_x, 13, 2, LANES), (rows, 4, LANES), (rows, 4, LANES), (columns, LANES)],
         [(rows, columns), decay_x.T.shape, decay_y.T.shape, (32, LANES), (rows, 4, LANES)],
         field,
         decay_x.T,
@@ -362,7 +367,7 @@
     got = exchange(sent, "gx", [list(range(along_x))], order_x)
     sent, wide = call(
         functools.partial(x_apply_y_ends, order=order_x),
-        [(blocks, 5, 8, LANES), (columns, LANES)],
+        [(blocks, 9, 4, LANES), (columns, LANES)],
         [
             (24, along_x, LANES),
             (along_x, 4, 4, LANES),
@@ -370,7 +375,7 @@
             (rows, 4, LANES),
             (columns, LANES),
         ],
-        got.reshape(along_x * 28, LANES),
+        got.reshape(along_x * 26, LANES),
         grid,
         ax,
         ay,
@@ -379,8 +384,8 @@
     got = exchange(sent, "gy", near, order_near)
     sent, own = call(
         functools.partial(y_join, order=order_near),
-        [(rows_y, 5, 8, LANES), (8, 8, LANES)],
-        [(blocks, 4, 8, LANES), (blocks, 4, 8, LANES)],
+        [(rows_y, 9, 4, LANES), (8, 8, LANES)],
+        [(blocks, 4, 8, LANES), (blocks, 4, 8, LANES), (blocks, 40, LANES)],
         got,
     )
     far = [[blocks * r + k for r in range(rows_y)] for k in range(blocks)]
@@ -388,7 +393,13 @@
     (out,) = call(
         functools.partial(y_apply, blocks=blocks, order=order_far),
         [(rows, columns)],
-        [(rows_y, 4, 8, LANES), (rows_y, 4, 8, LANES), (columns, LANES), (3, rows, LANES)],
+        [
+            (rows_y, 4, 8, LANES),
+            (rows_y, 4, 8, LANES),
+            (rows_y, 40, LANES),
+            (columns, LANES),
+            (3, rows, LANES),
+        ],
         got,
         own,
         wide,

time: 43.3 us -> 42.9 us (level)
  blocking collectives: 38.9 us -> 38.2 us
    all_to_all x3, blocking collectives: 38.9 us -> 38.2 us  [exchange(): lax.all_to_all(sent, axis, 0, 0, tiled=True, axis_index_groups=groups)]
where the time goes in v5:
time: 42.9 us; the launch traced here: 42.7 us
  blocking collectives  38.2 us (89%)
  Pallas kernels  4.49 us (10%)
    all_to_all x3, blocking collectives, exchange(): lax.all_to_all(sent, axis, 0, 0, tiled=True, axis_index_groups=groups)  38.2 us
    pallas_call x4, Pallas kernels, call(): pl.pallas_call(kernel, out_shape=[jax.ShapeDtypeStruct(shape, F32) for sh...  4.49 us

profile of v5, /device:TPU:4, one launch (start us, length us, event | category | flops | bytes accessed | tf_op | source)
XLA Modules:
  0.0 42.7 jit_solution(16528683900907351403)
XLA Ops:
  0.0 1.5 %shard_map.37 = (f32[16,13,2,128]{3,2,1,0:T(2,128)S(1)}, f32[64,4,128]{2,1,0:T(4,128)S(1)}, f32[64,4,128]{2,1,0:T(4,128)S(1)}, f32[384,128]{1,0:T(8,128)S(1)}) custom-call(f32[64,384]{1,0:T(8,128)} %field_ref.1, f32[8,64]{1,0:T(8,128)} %bitcast.4, f32[8,48]{1,0:T(8,128)} %bitcast.5), custom_call_target="tpu_custom_call" | custom-call | tf_op jit(solution)/shard_map/pallas_call | solution.py:325
  1.5 17.6 %all_to_all.15 = f32[16,13,2,128]{3,2,1,0:T(2,128)S(1)} all-to-all(f32[16,13,2,128]{3,2,1,0:T(2,128)S(1)} %get-tuple-element.13), channel_id=1, replica_groups={{416,160,384,128,480,224,448,192,32,288,0,256,96,352,64,320},{417,161,3..., dimensions={0} | all-to-all | bytes 425984 | tf_op jit(solution)/shard_map/all_to_all | solution.py:338
  19.2 1.1 %shard_map.38 = (f32[8,9,4,128]{3,2,1,0:T(4,128)S(1)}, f32[384,128]{1,0:T(8,128)S(1)}) custom-call(f32[416,128]{1,0:T(8,128)S(1)} %bitcast.3, f32[64,4,128]{2,1,0:T(4,128)S(1)} %get-tuple-element.14.grid_ref, f32[64,4,128]{2,1,0:T(4,128)S(1)} %get-tuple-element.15.ax_ref, f32[384,128]{1,0:T(8,128)S(1)} %get-tuple-element.16.ay_ref), custom_call_target="tpu_custom_call" | custom-call | tf_op jit(solution)/shard_map/pallas_call | solution.py:325
  20.2 12.5 %all_to_all.16.got_ref = f32[8,9,4,128]{3,2,1,0:T(4,128)S(1)} all-to-all(f32[8,9,4,128]{3,2,1,0:T(4,128)S(1)} %get-tuple-element.17), channel_id=1, replica_groups={{4,5,6,7,0,1,2,3},{12,13,14,15,8,9,10,11},{20,21,22,23,16,17,18,19},{28..., dimensions={0} | all-to-all | bytes 294912 | tf_op jit(solution)/shard_map/all_to_all | solution.py:338
  32.8 0.7 %shard_map.39 = (f32[4,9,4,128]{3,2,1,0:T(4,128)S(1)}, f32[8,8,128]{2,1,0:T(8,128)S(1)}) custom-call(f32[8,9,4,128]{3,2,1,0:T(4,128)S(1)} %all_to_all.16.got_ref), custom_call_target="tpu_custom_call" | custom-call | tf_op jit(solution)/shard_map/pallas_call | solution.py:325
  33.4 8.0 %all_to_all.17.got_ref = f32[4,9,4,128]{3,2,1,0:T(4,128)S(1)} all-to-all(f32[4,9,4,128]{3,2,1,0:T(4,128)S(1)} %get-tuple-element.18), channel_id=1, replica_groups={{16,24,0,8},{17,25,1,9},{18,26,2,10},{19,27,3,11},{20,28,4,12},{21,29,5..., dimensions={0} | all-to-all | bytes 147456 | tf_op jit(solution)/shard_map/all_to_all | solution.py:338
  41.5 1.2 %shard_map.40 = f32[64,384]{1,0:T(8,128)} custom-call(f32[4,9,4,128]{3,2,1,0:T(4,128)S(1)} %all_to_all.17.got_ref, f32[8,8,128]{2,1,0:T(8,128)S(1)} %get-tuple-element.19.mine_ref, f32[384,128]{1,0:T(8,128)S(1)} %get-tuple-element.20.wide_ref, f32[384,128]{1,0:T(8,128)S(1)} %get-tuple-element.16.ay_ref), custom_call_target="tpu_custom_call" | custom-call | tf_op jit(solution)/shard_map/pallas_call | solution.py:325

commit v6 on v5

--- a/solution.py
+++ b/solution.py
@@ -28,11 +28,14 @@
     return moved
 
 
-def toeplitz(column, states):
-    return [
-        sum((column[row - k] * states[k] for k in range(1, row + 1)), column[row] * states[0])
-        for row in range(4)
-    ]
+def toeplitz(column, states, added):
+    moved = []
+    for row in range(4):
+        total = added[row]
+        for k in range(row + 1):
+            total = total + column[row - k] * states[k]
+        moved.append(total)
+    return moved
 
 
 def sweep(steps, states, load, decay, gain, store, reverse):
@@ -79,7 +82,7 @@
         grid_ref[:, tile, :] = near_ref[:, tile * LANES : (tile + 1) * LANES]
     row, lane = (iota((4, LANES), 0), iota((4, LANES), 1))
     unit = [((row == tiles) & (lane // levels == k)).astype(F32) for k in range(8)]
-    chunk = 16
+    chunk = 64
 
     def ahead_steps(c, states):
         for step in range(chunk):
@@ -137,32 +140,34 @@
     return [part for tile in tiles for part in (tile[:4], tile[4:])] + [folded]
 
 
-def chained(got_ref, order, ahead, back, s_ref, t_ref, open_ref):
-    blocks, half = (got_ref.shape[0], LANES // 2)
+def chained(got_ref, order, ahead, back, s_ref, t_ref, maps_ref):
+    blocks, half = (s_ref.shape[0], LANES // 2)
     low = iota((8, LANES), 1) < half
+
+    def tile(m, k):
+        start = 36 * order.index(m) + 8 * k
+        return got_ref[start : start + 8, :]
+
     for place in range(blocks):
-        for k in range(9):
-            open_ref[place, 4 * k : 4 * k + 4, :] = got_ref[place, k]
-        open_ref[place, 36:40, :] = pltpu.roll(got_ref[place, 8], half, 1)
+        folded = got_ref[36 * place + 32 : 36 * place + 36, :]
+        maps_ref[place, :4, :] = folded
+        maps_ref[place, 4:, :] = pltpu.roll(folded, half, 1)
     for m in range(blocks):
-        at = order.index(m)
-        packed = open_ref[at, 32:40, :]
+        packed = maps_ref[order.index(m)]
         for k in range(4):
             s_ref[m, k] = ahead[k]
-        moved = toeplitz([lane_of(packed, 16 * k + 8) for k in range(4)], ahead)
-        ahead = [moved[k] + jnp.where(low, open_ref[at, 8 * k : 8 * k + 8, :], 0.0) for k in range(4)]
+        ends = [jnp.where(low, tile(m, k), 0.0) for k in range(4)]
+        ahead = toeplitz([lane_of(packed, 16 * k + 8) for k in range(4)], ahead, ends)
     for m in reversed(range(blocks)):
-        at = order.index(m)
-        packed = open_ref[at, 32:40, :]
+        packed = maps_ref[order.index(m)]
         for k in range(4):
             t_ref[m, k] = back[k]
-        moved = toeplitz([lane_of(packed, 16 * k + 4) for k in range(4)], back)
         turned = [
             sum(lane_of(packed, 16 * r + k) * s_ref[m, k] for k in range(4))
-            + jnp.where(low, pltpu.roll(open_ref[at, 8 * r : 8 * r + 8, :], half, 1), 0.0)
+            + jnp.where(low, pltpu.roll(tile(m, r), half, 1), 0.0)
             for r in range(4)
         ]
-        back = [moved[k] + turned[k] for k in range(4)]
+        back = toeplitz([lane_of(packed, 16 * k + 4) for k in range(4)], back, turned)
     return ahead, back
 
 
@@ -206,19 +211,18 @@
         for k in range(4):
             s_ref[m, k] = states[k]
         if m < devices - 1:
-            moved = toeplitz([entry(16 + k, m) for k in range(4)], states)
-            states = [moved[k] + end(m, k) for k in range(4)]
+            column = [entry(16 + k, m) for k in range(4)]
+            states = toeplitz(column, states, [end(m, k) for k in range(4)])
     states = [zero] * 4
     for m in reversed(range(devices)):
         for k in range(4):
             t_ref[m, k] = states[k]
         if m > 0:
-            moved = toeplitz([entry(20 + k, m) for k in range(4)], states)
             turned = [
                 sum(entry(4 * r + k, m) * s_ref[m, k] for k in range(4)) + end(m, 4 + r)
                 for r in range(4)
             ]
-            states = [moved[k] + turned[k] for k in range(4)]
+            states = toeplitz([entry(20 + k, m) for k in range(4)], states, turned)
     load_a = lambda i: ax_ref[i]
     gain = lambda i: 1.0 - ax_ref[i]
 
@@ -251,11 +255,11 @@
             sent_ref[device, k] = tiles[k]
 
 
-def y_join(got_ref, sent_ref, mine_ref, s_ref, t_ref, open_ref, *, order):
-    blocks = got_ref.shape[0]
+def y_join(got_ref, sent_ref, mine_ref, s_ref, t_ref, maps_ref, *, order):
+    blocks = s_ref.shape[0]
     lane = iota((8, LANES), 1)
     unit = [(lane == LANES // 2 + k).astype(F32) for k in range(8)]
-    ahead, back = chained(got_ref, order, unit[:4], unit[4:], s_ref, t_ref, open_ref)
+    ahead, back = chained(got_ref, order, unit[:4], unit[4:], s_ref, t_ref, maps_ref)
     tiles = pack(ahead, back, lane)
     for device in range(sent_ref.shape[0]):
         for k in range(9):
@@ -274,7 +278,7 @@
     field_ref,
     s_ref,
     t_ref,
-    open_ref,
+    maps_ref,
     z_ref,
     done_ref,
     sems,
@@ -284,7 +288,7 @@
 ):
     half = LANES // 2
     zero = [jnp.zeros((8, LANES), F32)] * 4
-    chained(got_ref, order, zero, zero, s_ref, t_ref, open_ref)
+    chained(got_ref, order, zero, zero, s_ref, t_ref, maps_ref)
     mine = lax.axis_index("gy") // blocks
     ahead = [s_ref[mine, k] for k in range(4)]
     back = [t_ref[mine, k] for k in range(4)]
@@ -385,8 +389,8 @@
     sent, own = call(
         functools.partial(y_join, order=order_near),
         [(rows_y, 9, 4, LANES), (8, 8, LANES)],
-        [(blocks, 4, 8, LANES), (blocks, 4, 8, LANES), (blocks, 40, LANES)],
-        got,
+        [(blocks, 4, 8, LANES), (blocks, 4, 8, LANES), (blocks, 8, LANES)],
+        got.reshape(blocks * 36, LANES),
     )
     far = [[blocks * r + k for r in range(rows_y)] for k in range(blocks)]
     got = exchange(sent, "gy", far, order_far)
@@ -396,11 +400,11 @@
         [
             (rows_y, 4, 8, LANES),
             (rows_y, 4, 8, LANES),
-            (rows_y, 40, LANES),
+            (rows_y, 8, LANES),
             (columns, LANES),
             (3, rows, LANES),
         ],
-        got,
+        got.reshape(rows_y * 36, LANES),
         own,
         wide,
         ay,

time: 42.9 us -> 42.8 us (level)
  no operation moved by 1% of the time
where the time goes in v6:
time: 42.8 us; the launch traced here: 42.6 us
  blocking collectives  38.2 us (89%)
  Pallas kernels  4.34 us (10%)
    all_to_all x3, blocking collectives, exchange(): lax.all_to_all(sent, axis, 0, 0, tiled=True, axis_index_groups=groups)  38.2 us
    pallas_call x4, Pallas kernels, call(): pl.pallas_call(kernel, out_shape=[jax.ShapeDtypeStruct(shape, F32) for sh...  4.34 us

profile of v6, /device:TPU:4, one launch (start us, length us, event | category | flops | bytes accessed | tf_op | source)
XLA Modules:
  0.0 42.6 jit_solution(5182018574494927779)
XLA Ops:
  0.0 1.4 %shard_map.37 = (f32[16,13,2,128]{3,2,1,0:T(2,128)S(1)}, f32[64,4,128]{2,1,0:T(4,128)S(1)}, f32[64,4,128]{2,1,0:T(4,128)S(1)}, f32[384,128]{1,0:T(8,128)S(1)}) custom-call(f32[64,384]{1,0:T(8,128)} %field_ref.1, f32[8,64]{1,0:T(8,128)} %bitcast.8, f32[8,48]{1,0:T(8,128)} %bitcast.9), custom_call_target="tpu_custom_call" | custom-call | tf_op jit(solution)/shard_map/pallas_call | solution.py:329
  1.4 17.6 %all_to_all.15 = f32[16,13,2,128]{3,2,1,0:T(2,128)S(1)} all-to-all(f32[16,13,2,128]{3,2,1,0:T(2,128)S(1)} %get-tuple-element.13), channel_id=1, replica_groups={{416,160,384,128,480,224,448,192,32,288,0,256,96,352,64,320},{417,161,3..., dimensions={0} | all-to-all | bytes 425984 | tf_op jit(solution)/shard_map/all_to_all | solution.py:342
  19.1 1.1 %shard_map.38 = (f32[8,9,4,128]{3,2,1,0:T(4,128)S(1)}, f32[384,128]{1,0:T(8,128)S(1)}) custom-call(f32[416,128]{1,0:T(8,128)S(1)} %bitcast.5, f32[64,4,128]{2,1,0:T(4,128)S(1)} %get-tuple-element.14.grid_ref, f32[64,4,128]{2,1,0:T(4,128)S(1)} %get-tuple-element.15.ax_ref, f32[384,128]{1,0:T(8,128)S(1)} %get-tuple-element.16.ay_ref), custom_call_target="tpu_custom_call" | custom-call | tf_op jit(solution)/shard_map/pallas_call | solution.py:329
  20.2 12.5 %all_to_all.16 = f32[8,9,4,128]{3,2,1,0:T(4,128)S(1)} all-to-all(f32[8,9,4,128]{3,2,1,0:T(4,128)S(1)} %get-tuple-element.17), channel_id=1, replica_groups={{4,5,6,7,0,1,2,3},{12,13,14,15,8,9,10,11},{20,21,22,23,16,17,18,19},{28..., dimensions={0} | all-to-all | bytes 294912 | tf_op jit(solution)/shard_map/all_to_all | solution.py:342
  32.7 0.7 %shard_map.39 = (f32[4,9,4,128]{3,2,1,0:T(4,128)S(1)}, f32[8,8,128]{2,1,0:T(8,128)S(1)}) custom-call(f32[288,128]{1,0:T(8,128)S(1)} %bitcast.6), custom_call_target="tpu_custom_call" | custom-call | tf_op jit(solution)/shard_map/pallas_call | solution.py:329
  33.4 8.0 %all_to_all.17 = f32[4,9,4,128]{3,2,1,0:T(4,128)S(1)} all-to-all(f32[4,9,4,128]{3,2,1,0:T(4,128)S(1)} %get-tuple-element.18), channel_id=1, replica_groups={{16,24,0,8},{17,25,1,9},{18,26,2,10},{19,27,3,11},{20,28,4,12},{21,29,5..., dimensions={0} | all-to-all | bytes 147456 | tf_op jit(solution)/shard_map/all_to_all | solution.py:342
  41.4 1.2 %shard_map.40 = f32[64,384]{1,0:T(8,128)} custom-call(f32[144,128]{1,0:T(8,128)S(1)} %bitcast.7, f32[8,8,128]{2,1,0:T(8,128)S(1)} %get-tuple-element.19.mine_ref, f32[384,128]{1,0:T(8,128)S(1)} %get-tuple-element.20.wide_ref, f32[384,128]{1,0:T(8,128)S(1)} %get-tuple-element.16.ay_ref), custom_call_target="tpu_custom_call" | custom-call | tf_op jit(solution)/shard_map/pallas_call | solution.py:329

commit v7 on v6

--- a/solution.py
+++ b/solution.py
@@ -62,11 +62,14 @@
     sems,
 ):
     levels, steps = decay_ref.shape
-    tiles = field_ref.shape[1] // LANES
+    tiles, half = (field_ref.shape[1] // LANES, steps // 2)
     copies = [
         pltpu.make_async_copy(decay_ref, short_ref, sems.at[0]),
         pltpu.make_async_copy(other_ref, turned_ref, sems.at[1]),
-        pltpu.make_async_copy(field_ref, near_ref, sems.at[2]),
+        *(
+            pltpu.make_async_copy(field_ref.at[part], near_ref.at[part], sems.at[2 + k])
+            for k, part in enumerate((pl.ds(0, half), pl.ds(half, half)))
+        ),
     ]
     for copy in copies:
         copy.start()
@@ -77,20 +80,9 @@
     grid_ref[:, tiles, :] = jnp.zeros((steps, LANES), F32)
     copies[1].wait()
     y_decays(turned_ref, ay_ref)
-    copies[2].wait()
-    for tile in range(tiles):
-        grid_ref[:, tile, :] = near_ref[:, tile * LANES : (tile + 1) * LANES]
     row, lane = (iota((4, LANES), 0), iota((4, LANES), 1))
     unit = [((row == tiles) & (lane // levels == k)).astype(F32) for k in range(8)]
-    chunk = 64
-
-    def ahead_steps(c, states):
-        for step in range(chunk):
-            i = c * chunk + step
-            a = a_ref[i]
-            states = cascade(states, grid_ref[i], a, 1.0 - a)
-            out_ref[i] = states[3]
-        return tuple(states)
+    chunk = steps
 
     def back_steps(c, states):
         for step in range(chunk):
@@ -99,22 +91,32 @@
             states = cascade(states, out_ref[i], a, 1.0 - a)
         return tuple(states)
 
-    ahead = lax.fori_loop(0, steps // chunk, ahead_steps, tuple(unit[:4]))
+    ahead = tuple(unit[:4])
+    for k in range(2):
+        copies[2 + k].wait()
+        part = slice(k * half, (k + 1) * half)
+        for tile in range(tiles):
+            grid_ref[part, tile, :] = near_ref[part, tile * LANES : (tile + 1) * LANES]
+        for i in range(k * half, (k + 1) * half):
+            a = a_ref[i]
+            ahead = tuple(cascade(ahead, grid_ref[i], a, 1.0 - a))
+            out_ref[i] = ahead[3]
     back = lax.fori_loop(0, steps // chunk, back_steps, tuple(unit[4:]))
-    for k, end in enumerate(ahead + back):
-        wide_ref[tiles * k : tiles * (k + 1), :] = end[:tiles]
     first = second = jnp.zeros((4, LANES), F32)
     for k in range(4):
         first += pltpu.roll(jnp.where(lane < 32, back[k], 0.0), 32 * k, 1)
         second += pltpu.roll(jnp.where(lane < 8, ahead[k], 0.0), 16 * k, 1)
         own = jnp.where((lane >= 32) & (lane < 40), back[k], 0.0)
         second += pltpu.roll(own, (16 * k - 24) % LANES, 1)
-    wide_ref[24:25, :] = first[tiles:]
-    wide_ref[25:26, :] = second[tiles:]
-    for part in range(sent_ref.shape[1]):
-        rows = wide_ref[2 * part : 2 * part + 2, :]
-        for device in range(sent_ref.shape[0]):
-            sent_ref[device, part] = rows
+    for start in range(0, wide_ref.shape[0], 26):
+        for k, end in enumerate(ahead + back):
+            wide_ref[start + tiles * k : start + tiles * (k + 1), :] = end[:tiles]
+        wide_ref[start + 24 : start + 25, :] = first[tiles:]
+        wide_ref[start + 25 : start + 26, :] = second[tiles:]
+    for place in range(wide_ref.shape[0] // 8):
+        rows = wide_ref[8 * place : 8 * place + 8, :]
+        for start in range(8 * place, sent_ref.shape[0], wide_ref.shape[0]):
+            sent_ref[start : start + 8, :] = rows
 
 
 def y_decays(decay_ref, a_ref):
@@ -360,14 +362,15 @@
     rows, columns = field.shape
     sent, grid, ax, ay = call(
         x_ends,
-        [(along_x, 13, 2, LANES), (rows, 4, LANES), (rows, 4, LANES), (columns, LANES)],
-        [(rows, columns), decay_x.T.shape, decay_y.T.shape, (32, LANES), (rows, 4, LANES)],
+        [(along_x * 26, LANES), (rows, 4, LANES), (rows, 4, LANES), (columns, LANES)],
+        [(rows, columns), decay_x.T.shape, decay_y.T.shape, (4 * 26, LANES), (rows, 4, LANES)],
         field,
         decay_x.T,
         decay_y.T,
         away_in=3,
-        sems=3,
+        sems=4,
     )
+    sent = sent.reshape(along_x, 13, 2, LANES)
     got = exchange(sent, "gx", [list(range(along_x))], order_x)
     sent, wide = call(
         functools.partial(x_apply_y_ends, order=order_x),

time: 42.8 us -> 42.8 us (level)
  no operation moved by 1% of the time
where the time goes in v7:
time: 42.8 us; the launch traced here: 42.6 us
  blocking collectives  38.2 us (89%)
  Pallas kernels  4.36 us (10%)
    all_to_all x3, blocking collectives, exchange(): lax.all_to_all(sent, axis, 0, 0, tiled=True, axis_index_groups=groups)  38.2 us
    pallas_call x4, Pallas kernels, call(): pl.pallas_call(kernel, out_shape=[jax.ShapeDtypeStruct(shape, F32) for sh...  4.36 us

profile of v7, /device:TPU:4, one launch (start us, length us, event | category | flops | bytes accessed | tf_op | source)
XLA Modules:
  0.0 42.6 jit_solution(1719373064347794171)
XLA Ops:
  0.0 1.5 %shard_map.37 = (f32[416,128]{1,0:T(8,128)S(1)}, f32[64,4,128]{2,1,0:T(4,128)S(1)}, f32[64,4,128]{2,1,0:T(4,128)S(1)}, f32[384,128]{1,0:T(8,128)S(1)}) custom-call(f32[64,384]{1,0:T(8,128)} %field_ref.1, f32[8,64]{1,0:T(8,128)} %bitcast.10, f32[8,48]{1,0:T(8,128)} %bitcast.11), custom_call_target="tpu_custom_call" | custom-call | tf_op jit(solution)/shard_map/pallas_call | solution.py:331
  1.5 17.6 %all_to_all.15 = f32[16,13,2,128]{3,2,1,0:T(2,128)S(1)} all-to-all(f32[16,13,2,128]{3,2,1,0:T(2,128)S(1)} %bitcast.9), channel_id=1, replica_groups={{416,160,384,128,480,224,448,192,32,288,0,256,96,352,64,320},{417,161,3..., dimensions={0} | all-to-all | bytes 425984 | tf_op jit(solution)/shard_map/all_to_all | solution.py:344
  19.1 1.1 %shard_map.38 = (f32[8,9,4,128]{3,2,1,0:T(4,128)S(1)}, f32[384,128]{1,0:T(8,128)S(1)}) custom-call(f32[416,128]{1,0:T(8,128)S(1)} %bitcast.6, f32[64,4,128]{2,1,0:T(4,128)S(1)} %get-tuple-element.14.grid_ref, f32[64,4,128]{2,1,0:T(4,128)S(1)} %get-tuple-element.15.ax_ref, f32[384,128]{1,0:T(8,128)S(1)} %get-tuple-element.16.ay_ref), custom_call_target="tpu_custom_call" | custom-call | tf_op jit(solution)/shard_map/pallas_call | solution.py:331
  20.2 12.5 %all_to_all.16 = f32[8,9,4,128]{3,2,1,0:T(4,128)S(1)} all-to-all(f32[8,9,4,128]{3,2,1,0:T(4,128)S(1)} %get-tuple-element.17), channel_id=1, replica_groups={{4,5,6,7,0,1,2,3},{12,13,14,15,8,9,10,11},{20,21,22,23,16,17,18,19},{28..., dimensions={0} | all-to-all | bytes 294912 | tf_op jit(solution)/shard_map/all_to_all | solution.py:344
  32.7 0.7 %shard_map.39 = (f32[4,9,4,128]{3,2,1,0:T(4,128)S(1)}, f32[8,8,128]{2,1,0:T(8,128)S(1)}) custom-call(f32[288,128]{1,0:T(8,128)S(1)} %bitcast.7), custom_call_target="tpu_custom_call" | custom-call | tf_op jit(solution)/shard_map/pallas_call | solution.py:331
  33.4 8.0 %all_to_all.17 = f32[4,9,4,128]{3,2,1,0:T(4,128)S(1)} all-to-all(f32[4,9,4,128]{3,2,1,0:T(4,128)S(1)} %get-tuple-element.18), channel_id=1, replica_groups={{16,24,0,8},{17,25,1,9},{18,26,2,10},{19,27,3,11},{20,28,4,12},{21,29,5..., dimensions={0} | all-to-all | bytes 147456 | tf_op jit(solution)/shard_map/all_to_all | solution.py:344
  41.4 1.2 %shard_map.40 = f32[64,384]{1,0:T(8,128)} custom-call(f32[144,128]{1,0:T(8,128)S(1)} %bitcast.8, f32[8,8,128]{2,1,0:T(8,128)S(1)} %get-tuple-element.19.mine_ref, f32[384,128]{1,0:T(8,128)S(1)} %get-tuple-element.20.wide_ref, f32[384,128]{1,0:T(8,128)S(1)} %get-tuple-element.16.ay_ref), custom_call_target="tpu_custom_call" | custom-call | tf_op jit(solution)/shard_map/pallas_call | solution.py:331

commit v8 on v6

--- a/solution.py
+++ b/solution.py
@@ -233,9 +233,10 @@
     sweep(steps, start, lambda i: grid_ref[i], load_a, gain, keep, False)
     start = [t_ref[mine, k] for k in range(4)]
     sweep(steps, start, lambda i: z_ref[i], load_a, gain, keep, True)
-    wide_ref[...] = jnp.zeros(wide_ref.shape, F32)
+    empty = jnp.zeros((LANES - steps, LANES), F32)
     for tile in range(3):
-        wide_ref[tile * LANES : (tile + 1) * LANES, :steps] = z_ref[:, tile, :].T
+        padded = jnp.concatenate([z_ref[:, tile, :], empty], axis=0)
+        wide_ref[tile * LANES : (tile + 1) * LANES, :] = padded.T
 
     lane = iota((8, LANES), 1)
     unit = [(lane == steps + k).astype(F32) for k in range(8)]

time: 42.8 us -> 42.8 us (level)
  no operation moved by 1% of the time
where the time goes in v8:
time: 42.8 us; the launch traced here: 42.5 us
  blocking collectives  38.2 us (89%)
  Pallas kernels  4.32 us (10%)
    all_to_all x3, blocking collectives, exchange(): lax.all_to_all(sent, axis, 0, 0, tiled=True, axis_index_groups=groups)  38.2 us
    pallas_call x4, Pallas kernels, call(): pl.pallas_call(kernel, out_shape=[jax.ShapeDtypeStruct(shape, F32) for sh...  4.32 us

profile of v8, /device:TPU:4, one launch (start us, length us, event | category | flops | bytes accessed | tf_op | source)
XLA Modules:
  0.0 42.5 jit_solution(17436743951907526607)
XLA Ops:
  0.0 1.4 %shard_map.37 = (f32[16,13,2,128]{3,2,1,0:T(2,128)S(1)}, f32[64,4,128]{2,1,0:T(4,128)S(1)}, f32[64,4,128]{2,1,0:T(4,128)S(1)}, f32[384,128]{1,0:T(8,128)S(1)}) custom-call(f32[64,384]{1,0:T(8,128)} %field_ref.1, f32[8,64]{1,0:T(8,128)} %bitcast.8, f32[8,48]{1,0:T(8,128)} %bitcast.9), custom_call_target="tpu_custom_call" | custom-call | tf_op jit(solution)/shard_map/pallas_call | solution.py:330
  1.4 17.6 %all_to_all.15 = f32[16,13,2,128]{3,2,1,0:T(2,128)S(1)} all-to-all(f32[16,13,2,128]{3,2,1,0:T(2,128)S(1)} %get-tuple-element.13), channel_id=1, replica_groups={{416,160,384,128,480,224,448,192,32,288,0,256,96,352,64,320},{417,161,3..., dimensions={0} | all-to-all | bytes 425984 | tf_op jit(solution)/shard_map/all_to_all | solution.py:343
  19.1 1.1 %shard_map.38 = (f32[8,9,4,128]{3,2,1,0:T(4,128)S(1)}, f32[384,128]{1,0:T(8,128)S(1)}) custom-call(f32[416,128]{1,0:T(8,128)S(1)} %bitcast.5, f32[64,4,128]{2,1,0:T(4,128)S(1)} %get-tuple-element.14.grid_ref, f32[64,4,128]{2,1,0:T(4,128)S(1)} %get-tuple-element.15.ax_ref, f32[384,128]{1,0:T(8,128)S(1)} %get-tuple-element.16.ay_ref), custom_call_target="tpu_custom_call" | custom-call | tf_op jit(solution)/shard_map/pallas_call | solution.py:330
  20.2 12.5 %all_to_all.16 = f32[8,9,4,128]{3,2,1,0:T(4,128)S(1)} all-to-all(f32[8,9,4,128]{3,2,1,0:T(4,128)S(1)} %get-tuple-element.17), channel_id=1, replica_groups={{4,5,6,7,0,1,2,3},{12,13,14,15,8,9,10,11},{20,21,22,23,16,17,18,19},{28..., dimensions={0} | all-to-all | bytes 294912 | tf_op jit(solution)/shard_map/all_to_all | solution.py:343
  32.7 0.7 %shard_map.39 = (f32[4,9,4,128]{3,2,1,0:T(4,128)S(1)}, f32[8,8,128]{2,1,0:T(8,128)S(1)}) custom-call(f32[288,128]{1,0:T(8,128)S(1)} %bitcast.6), custom_call_target="tpu_custom_call" | custom-call | tf_op jit(solution)/shard_map/pallas_call | solution.py:330
  33.3 8.0 %all_to_all.17 = f32[4,9,4,128]{3,2,1,0:T(4,128)S(1)} all-to-all(f32[4,9,4,128]{3,2,1,0:T(4,128)S(1)} %get-tuple-element.18), channel_id=1, replica_groups={{16,24,0,8},{17,25,1,9},{18,26,2,10},{19,27,3,11},{20,28,4,12},{21,29,5..., dimensions={0} | all-to-all | bytes 147456 | tf_op jit(solution)/shard_map/all_to_all | solution.py:343
  41.4 1.2 %shard_map.40 = f32[64,384]{1,0:T(8,128)} custom-call(f32[144,128]{1,0:T(8,128)S(1)} %bitcast.7, f32[8,8,128]{2,1,0:T(8,128)S(1)} %get-tuple-element.19.mine_ref, f32[384,128]{1,0:T(8,128)S(1)} %get-tuple-element.20.wide_ref, f32[384,128]{1,0:T(8,128)S(1)} %get-tuple-element.16.ay_ref), custom_call_target="tpu_custom_call" | custom-call | tf_op jit(solution)/shard_map/pallas_call | solution.py:330
